TPU v7x, 32 devices: a whole 2x2x4 slice. The times are simulated.
32 devices in a mesh: grp: 8 (over z, core), dom: 4 (over y, x).
Axes of the slice: x: 2, y: 2, z: 4, core: 2. Of those that a mesh axis runs over, the one named last changes fastest.
Arguments:
- connect: int32 [20, 4096], P(None, ('grp', 'dom')), may hold values from 0 to 511, as said below
- interface_nodes: int32 [32, 4, 32], P(('grp', 'dom')), may hold values from 0 to 511, as said below
- neighbours: int32 [32, 4], P(('grp', 'dom')), may hold values from 0 to 1, as said below
- point_rank: int32 [32, 2048], P(('grp', 'dom')), may hold values from 0 to 2047, each once within a row
- shape_grad: float32 [48, 20], replicated, may hold values from -1.25 to 1.25
- inverse_jacobian: float32 [9, 4096], P(None, ('grp', 'dom')), may hold values from -0.45 to 2.5
- lame_moduli: float32 [2, 4096], P(None, ('grp', 'dom')), may hold values from 0.5 to 2
- point_weights: float32 [16, 4096], P(None, ('grp', 'dom')), may hold values from 0.003 to 0.02
- mass_elem: float32 [20, 4096], P(None, ('grp', 'dom')), may hold values from 0.5 to 2
- source_pattern: float32 [3, 16384], P(None, ('grp', 'dom')), may hold values from -6 to 6
- wavelet: float32 [16], replicated, may hold values from -6 to 6
Outputs:
- strain_db: bfloat16 [16, 6, 65536], P(None, None, ('grp', 'dom'))
Inputs may be any that keep to these rules, and one draw needn't show every extreme that they name: `connect`: every one of a partition's 512 nodes is named by some element of that partition. `interface_nodes`: entry i of list k of a partition and entry i of the opposite list of the partition beside it in direction k are copies of one node; no node stands twice among a partition's four lists. `neighbours`: the entry of a partition in direction k equals that of the partition beside it in the opposite direction; it is 0 where no partition lies in direction k.
All inputs are finite; a program needn't handle non-finite values.
Results may differ from a plain program's by a relative error of at most 0.001.
Values may be sent and summed in bfloat16 or wider, within the bound.
A program may use at most 64 MiB of HBM per device.

v0:
```python
import jax
import jax.numpy as jnp
from jax import lax
from jax.sharding import PartitionSpec as P

EL_NODES = 20
POINTS = 16
STRAIN = 6
STEPS = 16


time_step = 0.5


def extended(cells, sides, width):
    for axis, dim in sides:
        count = lax.axis_size(axis)
        ends = count - 1
        head = lax.slice_in_dim(cells, 0, width, axis=dim)
        tail = lax.slice_in_dim(cells, cells.shape[dim] - width, cells.shape[dim], axis=dim)
        cells = jnp.concatenate(
            [
                lax.ppermute(tail, axis, [(i, (i + 1) % count) for i in range(ends)]),
                cells,
                lax.ppermute(head, axis, [((i + 1) % count, i) for i in range(ends)]),
            ],
            axis=dim,
        )
    return cells


def gather_nodes(displace, incidence, elements):
    node_values = lax.dot_general(
        displace,
        incidence.astype(jnp.float32),
        (((1,), (1,)), ((), ())),
        precision=lax.Precision.HIGHEST,
        preferred_element_type=jnp.float32,
    )
    return node_values.reshape(displace.shape[0], EL_NODES, elements)


def scatter_nodes(node_values, incidence):
    flat = node_values.reshape(node_values.shape[0], -1)
    return jnp.dot(
        flat,
        incidence.astype(jnp.float32),
        precision=lax.Precision.HIGHEST,
        preferred_element_type=jnp.float32,
    )


def gradient_at(displace, incidence, shape_grad, inverse_jacobian):
    elements = inverse_jacobian.shape[1]
    node_values = gather_nodes(displace, incidence, elements)
    along_ref = jnp.einsum("mn,cne->cme", shape_grad, node_values, precision=lax.Precision.HIGHEST)
    along_ref = along_ref.reshape(3, 3, POINTS, elements)
    jacobian = inverse_jacobian.reshape(3, 3, elements)
    result = along_ref[:, 0, None] * jacobian[0][None, :, None, :]
    result = result + along_ref[:, 1, None] * jacobian[1][None, :, None, :]
    result = result + along_ref[:, 2, None] * jacobian[2][None, :, None, :]
    return result


def strain_of(tensor):
    return jnp.stack(
        [
            tensor[0, 0],
            tensor[1, 1],
            tensor[2, 2],
            0.5 * (tensor[1, 2] + tensor[2, 1]),
            0.5 * (tensor[0, 2] + tensor[2, 0]),
            0.5 * (tensor[0, 1] + tensor[1, 0]),
        ],
        axis=0,
    )


def element_forces(tensor, lame_moduli, point_weights, inverse_jacobian, shape_grad, incidence):
    elements = inverse_jacobian.shape[1]
    jacobian = inverse_jacobian.reshape(3, 3, elements)
    volume_change = tensor[0, 0] + tensor[1, 1] + tensor[2, 2]
    identity = jnp.eye(3, dtype=jnp.float32)
    stress = lame_moduli[1][None, None, None, :] * (tensor + tensor.transpose(1, 0, 2, 3))
    stress = (
        stress + identity[:, :, None, None] * (lame_moduli[0][None, :] * volume_change)[None, None]
    )
    mapped = stress[:, 0][:, None] * jacobian[:, 0][None, :, None, :]
    mapped = mapped + stress[:, 1][:, None] * jacobian[:, 1][None, :, None, :]
    mapped = mapped + stress[:, 2][:, None] * jacobian[:, 2][None, :, None, :]
    mapped = mapped * point_weights[None, None]
    node_values = jnp.einsum(
        "mn,cme->cne",
        shape_grad,
        mapped.reshape(3, 3 * POINTS, elements),
        precision=lax.Precision.HIGHEST,
    )
    return scatter_nodes(node_values, incidence)


def shards(
    connect,
    interface_nodes,
    neighbours,
    point_rank,
    shape_grad,
    inverse_jacobian,
    lame_moduli,
    point_weights,
    mass_elem,
    source_pattern,
    wavelet,
):
    node_count = source_pattern.shape[1]
    elements = connect.shape[1]
    point_count = point_rank.shape[1]
    shared_nodes = interface_nodes[0]
    neighbour_mask = neighbours[0].astype(jnp.float32)
    node_ids = jnp.arange(node_count, dtype=jnp.int32)
    incidence = (connect.reshape(-1)[:, None] == node_ids[None, :]).astype(jnp.bfloat16)

    def assemble(node_field):
        picked = jnp.take(node_field, shared_nodes, axis=1)
        lower_upper = extended(picked[:, 0:2], (("grp", 1),), 1)
        left_right = extended(picked[:, 2:4], (("dom", 1),), 1)
        received = jnp.concatenate(
            [lower_upper[:, 0:1], lower_upper[:, 3:4], left_right[:, 0:1], left_right[:, 3:4]],
            axis=1,
        )
        return node_field.at[:, shared_nodes].add(received * neighbour_mask[None, :, None])

    node_mass = scatter_nodes(mass_elem[None], incidence)
    inverse_mass = 1.0 / assemble(node_mass)
    inverse_rank = (
        jnp.zeros((point_count,), jnp.int32)
        .at[point_rank[0]]
        .set(jnp.arange(point_count, dtype=jnp.int32))
    )

    def record_strain(strain_store, slot_index, tensor):
        snapshot = strain_of(tensor).reshape(STRAIN, point_count).astype(jnp.bfloat16)
        return lax.dynamic_update_slice(strain_store, snapshot[None], (slot_index, 0, 0))

    def advance(step_index, loop_state):
        displace, velocity, tensor, strain_store = loop_state
        force = wavelet[step_index] * source_pattern - element_forces(
            tensor, lame_moduli, point_weights, inverse_jacobian, shape_grad, incidence
        )
        force = assemble(force)
        velocity = velocity + time_step * inverse_mass * force
        displace = displace + time_step * velocity
        fresh = gradient_at(displace, incidence, shape_grad, inverse_jacobian)
        strain_store = record_strain(strain_store, step_index, fresh)
        return (displace, velocity, fresh, strain_store)

    start = jnp.zeros((3, node_count), jnp.float32)
    first_tensor = jnp.zeros((3, 3, POINTS, elements), jnp.float32)
    strain_store = jnp.zeros((STEPS, STRAIN, point_count), jnp.bfloat16)
    displace, velocity, tensor, strain_store = lax.fori_loop(
        0, STEPS, advance, (start, start, first_tensor, strain_store)
    )
    ordered = jnp.take(strain_store, inverse_rank, axis=2)
    strain_store = lax.all_to_all(ordered, "dom", split_axis=2, concat_axis=2, tiled=True)
    return strain_store


def solution(mesh):
    placed = (
        P(None, ("grp", "dom")),
        P(("grp", "dom"), None, None),
        P(("grp", "dom"), None),
        P(("grp", "dom"), None),
        P(),
        P(None, ("grp", "dom")),
        P(None, ("grp", "dom")),
        P(None, ("grp", "dom")),
        P(None, ("grp", "dom")),
        P(None, ("grp", "dom")),
        P(),
    )
    return jax.shard_map(
        shards, mesh=mesh, in_specs=placed, out_specs=P(None, None, ("grp", "dom")), check_vma=False
    )
```

profile of v0, /device:TPU:0, one launch (start us, length us, event | category | flops | bytes accessed | tf_op | source)
XLA Modules:
  0.0 452.5 jit_solution(3150810587636656340)
XLA Ops:
  9.8 4.8 %collective-permute-start.6 = (f32[1,1,32]{2,1,0:T(1,128)S(1)}, f32[1,1,32]{2,1,0:T(1,128)S(1)}, u32[]{:S(2)}, u32[]{:S(2)}) collective-permute-start(f32[1,1,32]{2,1,0:T(1,128)S(1)} %get-tuple-element.363), channel_id=1, source_target_pairs={{0,1},{1,2},{2,3},{4,5},{5,6},{6,7},{8,9},{9,10},{10,11},{12,13},{... | collective-permute-start | bytes 392 | tf_op jit(solution)/shard_map/ppermute | solution.py:23
  16.7 8.0 %scatter_custom_fusion.1 = s32[2048]{0:T(1024)S(1)} fusion(s32[2048]{0:T(1024)S(1)} %bitcast.217, s32[2048]{0:T(1024)S(1)} %iota.33, s32[]{:T(128)} %constant.94.clone.1), kind=kCustom, calls=%fused_computation.79 | custom fusion | bytes 8196 | tf_op jit(solution)/shard_map/scatter | solution.py:137
  27.9 367.5 %while.21 = (s32[]{:T(128)}, f32[3,512]{0,1:T(8,128)S(1)}, f32[3,512]{0,1:T(8,128)S(1)}, f32[3,3,16,128]{3,2,1,0:T(8,128)S(1)}, bf16[16,6,2048]{2,1,0:T(8,128)(2...) while((s32[]{:T(128)}, f32[3,512]{0,1:T(8,128)S(1)}, ...), condition=%wide.wide.region_4.5_spmd.clone, body=%wide.wide.region_2.4_spmd.clone.sunk | while | flops 108817296 | bytes 1922756 | solution.py:159
  33.3 5.4 %collective-permute-start.1 = (f32[3,1,32]{2,1,0:T(1,128)S(1)}, f32[3,1,32]{2,1,0:T(1,128)S(1)}, u32[]{:S(2)}, u32[]{:S(2)}) collective-permute-start(f32[3,1,32]{2,1,0:T(1,128)S(1)} %get-tuple-element.593), channel_id=1, source_target_pairs={{0,1},{1,2},{2,3},{4,5},{5,6},{6,7},{8,9},{9,10},{10,11},{12,13},{... | collective-permute-start | bytes 1160 | tf_op jit(solution)/shard_map/while/body/eval_jaxpr/ppermute | solution.py:23
  40.0 4.2 collective-permute-start.3
  46.8 3.0 fusion.109
  55.8 5.2 %collective-permute-start.1 = (f32[3,1,32]{2,1,0:T(1,128)S(1)}, f32[3,1,32]{2,1,0:T(1,128)S(1)}, u32[]{:S(2)}, u32[]{:S(2)}) collective-permute-start(f32[3,1,32]{2,1,0:T(1,128)S(1)} %get-tuple-element.593), channel_id=1, source_target_pairs={{0,1},{1,2},{2,3},{4,5},{5,6},{6,7},{8,9},{9,10},{10,11},{12,13},{... | collective-permute-start | bytes 1160 | tf_op jit(solution)/shard_map/while/body/eval_jaxpr/ppermute | solution.py:23
  62.2 4.5 collective-permute-start.3
  69.3 3.0 fusion.109
  78.2 5.2 %collective-permute-start.1 = (f32[3,1,32]{2,1,0:T(1,128)S(1)}, f32[3,1,32]{2,1,0:T(1,128)S(1)}, u32[]{:S(2)}, u32[]{:S(2)}) collective-permute-start(f32[3,1,32]{2,1,0:T(1,128)S(1)} %get-tuple-element.593), channel_id=1, source_target_pairs={{0,1},{1,2},{2,3},{4,5},{5,6},{6,7},{8,9},{9,10},{10,11},{12,13},{... | collective-permute-start | bytes 1160 | tf_op jit(solution)/shard_map/while/body/eval_jaxpr/ppermute | solution.py:23
  84.7 5.0 %collective-permute-start.3 = (f32[3,1,32]{2,1,0:T(1,128)S(1)}, f32[3,1,32]{2,1,0:T(1,128)S(1)}, u32[]{:S(2)}, u32[]{:S(2)}) collective-permute-start(f32[3,1,32]{2,1,0:T(1,128)S(1)} %get-tuple-element.595), channel_id=1, source_target_pairs={{0,4},{4,8},{8,12},{12,16},{16,20},{20,24},{24,28},{1,5},{5,9},{9,... | collective-permute-start | bytes 1160 | tf_op jit(solution)/shard_map/while/body/eval_jaxpr/ppermute | solution.py:23
  92.3 3.0 fusion.109
  101.3 5.2 %collective-permute-start.1 = (f32[3,1,32]{2,1,0:T(1,128)S(1)}, f32[3,1,32]{2,1,0:T(1,128)S(1)}, u32[]{:S(2)}, u32[]{:S(2)}) collective-permute-start(f32[3,1,32]{2,1,0:T(1,128)S(1)} %get-tuple-element.593), channel_id=1, source_target_pairs={{0,1},{1,2},{2,3},{4,5},{5,6},{6,7},{8,9},{9,10},{10,11},{12,13},{... | collective-permute-start | bytes 1160 | tf_op jit(solution)/shard_map/while/body/eval_jaxpr/ppermute | solution.py:23
  107.8 5.0 %collective-permute-start.3 = (f32[3,1,32]{2,1,0:T(1,128)S(1)}, f32[3,1,32]{2,1,0:T(1,128)S(1)}, u32[]{:S(2)}, u32[]{:S(2)}) collective-permute-start(f32[3,1,32]{2,1,0:T(1,128)S(1)} %get-tuple-element.595), channel_id=1, source_target_pairs={{0,4},{4,8},{8,12},{12,16},{16,20},{20,24},{24,28},{1,5},{5,9},{9,... | collective-permute-start | bytes 1160 | tf_op jit(solution)/shard_map/while/body/eval_jaxpr/ppermute | solution.py:23
  115.3 3.0 fusion.109
  124.3 5.2 %collective-permute-start.1 = (f32[3,1,32]{2,1,0:T(1,128)S(1)}, f32[3,1,32]{2,1,0:T(1,128)S(1)}, u32[]{:S(2)}, u32[]{:S(2)}) collective-permute-start(f32[3,1,32]{2,1,0:T(1,128)S(1)} %get-tuple-element.593), channel_id=1, source_target_pairs={{0,1},{1,2},{2,3},{4,5},{5,6},{6,7},{8,9},{9,10},{10,11},{12,13},{... | collective-permute-start | bytes 1160 | tf_op jit(solution)/shard_map/while/body/eval_jaxpr/ppermute | solution.py:23
  130.8 5.0 %collective-permute-start.3 = (f32[3,1,32]{2,1,0:T(1,128)S(1)}, f32[3,1,32]{2,1,0:T(1,128)S(1)}, u32[]{:S(2)}, u32[]{:S(2)}) collective-permute-start(f32[3,1,32]{2,1,0:T(1,128)S(1)} %get-tuple-element.595), channel_id=1, source_target_pairs={{0,4},{4,8},{8,12},{12,16},{16,20},{20,24},{24,28},{1,5},{5,9},{9,... | collective-permute-start | bytes 1160 | tf_op jit(solution)/shard_map/while/body/eval_jaxpr/ppermute | solution.py:23
  138.4 3.0 fusion.109
  147.4 5.2 %collective-permute-start.1 = (f32[3,1,32]{2,1,0:T(1,128)S(1)}, f32[3,1,32]{2,1,0:T(1,128)S(1)}, u32[]{:S(2)}, u32[]{:S(2)}) collective-permute-start(f32[3,1,32]{2,1,0:T(1,128)S(1)} %get-tuple-element.593), channel_id=1, source_target_pairs={{0,1},{1,2},{2,3},{4,5},{5,6},{6,7},{8,9},{9,10},{10,11},{12,13},{... | collective-permute-start | bytes 1160 | tf_op jit(solution)/shard_map/while/body/eval_jaxpr/ppermute | solution.py:23
  153.8 5.0 %collective-permute-start.3 = (f32[3,1,32]{2,1,0:T(1,128)S(1)}, f32[3,1,32]{2,1,0:T(1,128)S(1)}, u32[]{:S(2)}, u32[]{:S(2)}) collective-permute-start(f32[3,1,32]{2,1,0:T(1,128)S(1)} %get-tuple-element.595), channel_id=1, source_target_pairs={{0,4},{4,8},{8,12},{12,16},{16,20},{20,24},{24,28},{1,5},{5,9},{9,... | collective-permute-start | bytes 1160 | tf_op jit(solution)/shard_map/while/body/eval_jaxpr/ppermute | solution.py:23
  161.4 3.0 fusion.109
  170.4 5.2 %collective-permute-start.1 = (f32[3,1,32]{2,1,0:T(1,128)S(1)}, f32[3,1,32]{2,1,0:T(1,128)S(1)}, u32[]{:S(2)}, u32[]{:S(2)}) collective-permute-start(f32[3,1,32]{2,1,0:T(1,128)S(1)} %get-tuple-element.593), channel_id=1, source_target_pairs={{0,1},{1,2},{2,3},{4,5},{5,6},{6,7},{8,9},{9,10},{10,11},{12,13},{... | collective-permute-start | bytes 1160 | tf_op jit(solution)/shard_map/while/body/eval_jaxpr/ppermute | solution.py:23
  176.9 5.0 %collective-permute-start.3 = (f32[3,1,32]{2,1,0:T(1,128)S(1)}, f32[3,1,32]{2,1,0:T(1,128)S(1)}, u32[]{:S(2)}, u32[]{:S(2)}) collective-permute-start(f32[3,1,32]{2,1,0:T(1,128)S(1)} %get-tuple-element.595), channel_id=1, source_target_pairs={{0,4},{4,8},{8,12},{12,16},{16,20},{20,24},{24,28},{1,5},{5,9},{9,... | collective-permute-start | bytes 1160 | tf_op jit(solution)/shard_map/while/body/eval_jaxpr/ppermute | solution.py:23
  193.4 5.2 %collective-permute-start.1 = (f32[3,1,32]{2,1,0:T(1,128)S(1)}, f32[3,1,32]{2,1,0:T(1,128)S(1)}, u32[]{:S(2)}, u32[]{:S(2)}) collective-permute-start(f32[3,1,32]{2,1,0:T(1,128)S(1)} %get-tuple-element.593), channel_id=1, source_target_pairs={{0,1},{1,2},{2,3},{4,5},{5,6},{6,7},{8,9},{9,10},{10,11},{12,13},{... | collective-permute-start | bytes 1160 | tf_op jit(solution)/shard_map/while/body/eval_jaxpr/ppermute | solution.py:23
  199.9 5.0 %collective-permute-start.3 = (f32[3,1,32]{2,1,0:T(1,128)S(1)}, f32[3,1,32]{2,1,0:T(1,128)S(1)}, u32[]{:S(2)}, u32[]{:S(2)}) collective-permute-start(f32[3,1,32]{2,1,0:T(1,128)S(1)} %get-tuple-element.595), channel_id=1, source_target_pairs={{0,4},{4,8},{8,12},{12,16},{16,20},{20,24},{24,28},{1,5},{5,9},{9,... | collective-permute-start | bytes 1160 | tf_op jit(solution)/shard_map/while/body/eval_jaxpr/ppermute | solution.py:23
  216.5 5.2 %collective-permute-start.1 = (f32[3,1,32]{2,1,0:T(1,128)S(1)}, f32[3,1,32]{2,1,0:T(1,128)S(1)}, u32[]{:S(2)}, u32[]{:S(2)}) collective-permute-start(f32[3,1,32]{2,1,0:T(1,128)S(1)} %get-tuple-element.593), channel_id=1, source_target_pairs={{0,1},{1,2},{2,3},{4,5},{5,6},{6,7},{8,9},{9,10},{10,11},{12,13},{... | collective-permute-start | bytes 1160 | tf_op jit(solution)/shard_map/while/body/eval_jaxpr/ppermute | solution.py:23
  222.9 5.0 %collective-permute-start.3 = (f32[3,1,32]{2,1,0:T(1,128)S(1)}, f32[3,1,32]{2,1,0:T(1,128)S(1)}, u32[]{:S(2)}, u32[]{:S(2)}) collective-permute-start(f32[3,1,32]{2,1,0:T(1,128)S(1)} %get-tuple-element.595), channel_id=1, source_target_pairs={{0,4},{4,8},{8,12},{12,16},{16,20},{20,24},{24,28},{1,5},{5,9},{9,... | collective-permute-start | bytes 1160 | tf_op jit(solution)/shard_map/while/body/eval_jaxpr/ppermute | solution.py:23
  239.5 5.2 %collective-permute-start.1 = (f32[3,1,32]{2,1,0:T(1,128)S(1)}, f32[3,1,32]{2,1,0:T(1,128)S(1)}, u32[]{:S(2)}, u32[]{:S(2)}) collective-permute-start(f32[3,1,32]{2,1,0:T(1,128)S(1)} %get-tuple-element.593), channel_id=1, source_target_pairs={{0,1},{1,2},{2,3},{4,5},{5,6},{6,7},{8,9},{9,10},{10,11},{12,13},{... | collective-permute-start | bytes 1160 | tf_op jit(solution)/shard_map/while/body/eval_jaxpr/ppermute | solution.py:23
  246.0 5.0 %collective-permute-start.3 = (f32[3,1,32]{2,1,0:T(1,128)S(1)}, f32[3,1,32]{2,1,0:T(1,128)S(1)}, u32[]{:S(2)}, u32[]{:S(2)}) collective-permute-start(f32[3,1,32]{2,1,0:T(1,128)S(1)} %get-tuple-element.595), channel_id=1, source_target_pairs={{0,4},{4,8},{8,12},{12,16},{16,20},{20,24},{24,28},{1,5},{5,9},{9,... | collective-permute-start | bytes 1160 | tf_op jit(solution)/shard_map/while/body/eval_jaxpr/ppermute | solution.py:23
  262.5 5.2 %collective-permute-start.1 = (f32[3,1,32]{2,1,0:T(1,128)S(1)}, f32[3,1,32]{2,1,0:T(1,128)S(1)}, u32[]{:S(2)}, u32[]{:S(2)}) collective-permute-start(f32[3,1,32]{2,1,0:T(1,128)S(1)} %get-tuple-element.593), channel_id=1, source_target_pairs={{0,1},{1,2},{2,3},{4,5},{5,6},{6,7},{8,9},{9,10},{10,11},{12,13},{... | collective-permute-start | bytes 1160 | tf_op jit(solution)/shard_map/while/body/eval_jaxpr/ppermute | solution.py:23
  269.0 5.0 %collective-permute-start.3 = (f32[3,1,32]{2,1,0:T(1,128)S(1)}, f32[3,1,32]{2,1,0:T(1,128)S(1)}, u32[]{:S(2)}, u32[]{:S(2)}) collective-permute-start(f32[3,1,32]{2,1,0:T(1,128)S(1)} %get-tuple-element.595), channel_id=1, source_target_pairs={{0,4},{4,8},{8,12},{12,16},{16,20},{20,24},{24,28},{1,5},{5,9},{9,... | collective-permute-start | bytes 1160 | tf_op jit(solution)/shard_map/while/body/eval_jaxpr/ppermute | solution.py:23
  285.6 5.2 %collective-permute-start.1 = (f32[3,1,32]{2,1,0:T(1,128)S(1)}, f32[3,1,32]{2,1,0:T(1,128)S(1)}, u32[]{:S(2)}, u32[]{:S(2)}) collective-permute-start(f32[3,1,32]{2,1,0:T(1,128)S(1)} %get-tuple-element.593), channel_id=1, source_target_pairs={{0,1},{1,2},{2,3},{4,5},{5,6},{6,7},{8,9},{9,10},{10,11},{12,13},{... | collective-permute-start | bytes 1160 | tf_op jit(solution)/shard_map/while/body/eval_jaxpr/ppermute | solution.py:23
  292.0 5.0 %collective-permute-start.3 = (f32[3,1,32]{2,1,0:T(1,128)S(1)}, f32[3,1,32]{2,1,0:T(1,128)S(1)}, u32[]{:S(2)}, u32[]{:S(2)}) collective-permute-start(f32[3,1,32]{2,1,0:T(1,128)S(1)} %get-tuple-element.595), channel_id=1, source_target_pairs={{0,4},{4,8},{8,12},{12,16},{16,20},{20,24},{24,28},{1,5},{5,9},{9,... | collective-permute-start | bytes 1160 | tf_op jit(solution)/shard_map/while/body/eval_jaxpr/ppermute | solution.py:23
  308.6 5.2 %collective-permute-start.1 = (f32[3,1,32]{2,1,0:T(1,128)S(1)}, f32[3,1,32]{2,1,0:T(1,128)S(1)}, u32[]{:S(2)}, u32[]{:S(2)}) collective-permute-start(f32[3,1,32]{2,1,0:T(1,128)S(1)} %get-tuple-element.593), channel_id=1, source_target_pairs={{0,1},{1,2},{2,3},{4,5},{5,6},{6,7},{8,9},{9,10},{10,11},{12,13},{... | collective-permute-start | bytes 1160 | tf_op jit(solution)/shard_map/while/body/eval_jaxpr/ppermute | solution.py:23
  315.1 5.0 %collective-permute-start.3 = (f32[3,1,32]{2,1,0:T(1,128)S(1)}, f32[3,1,32]{2,1,0:T(1,128)S(1)}, u32[]{:S(2)}, u32[]{:S(2)}) collective-permute-start(f32[3,1,32]{2,1,0:T(1,128)S(1)} %get-tuple-element.595), channel_id=1, source_target_pairs={{0,4},{4,8},{8,12},{12,16},{16,20},{20,24},{24,28},{1,5},{5,9},{9,... | collective-permute-start | bytes 1160 | tf_op jit(solution)/shard_map/while/body/eval_jaxpr/ppermute | solution.py:23
  331.6 5.2 %collective-permute-start.1 = (f32[3,1,32]{2,1,0:T(1,128)S(1)}, f32[3,1,32]{2,1,0:T(1,128)S(1)}, u32[]{:S(2)}, u32[]{:S(2)}) collective-permute-start(f32[3,1,32]{2,1,0:T(1,128)S(1)} %get-tuple-element.593), channel_id=1, source_target_pairs={{0,1},{1,2},{2,3},{4,5},{5,6},{6,7},{8,9},{9,10},{10,11},{12,13},{... | collective-permute-start | bytes 1160 | tf_op jit(solution)/shard_map/while/body/eval_jaxpr/ppermute | solution.py:23
  338.1 5.0 %collective-permute-start.3 = (f32[3,1,32]{2,1,0:T(1,128)S(1)}, f32[3,1,32]{2,1,0:T(1,128)S(1)}, u32[]{:S(2)}, u32[]{:S(2)}) collective-permute-start(f32[3,1,32]{2,1,0:T(1,128)S(1)} %get-tuple-element.595), channel_id=1, source_target_pairs={{0,4},{4,8},{8,12},{12,16},{16,20},{20,24},{24,28},{1,5},{5,9},{9,... | collective-permute-start | bytes 1160 | tf_op jit(solution)/shard_map/while/body/eval_jaxpr/ppermute | solution.py:23
  354.7 5.2 %collective-permute-start.1 = (f32[3,1,32]{2,1,0:T(1,128)S(1)}, f32[3,1,32]{2,1,0:T(1,128)S(1)}, u32[]{:S(2)}, u32[]{:S(2)}) collective-permute-start(f32[3,1,32]{2,1,0:T(1,128)S(1)} %get-tuple-element.593), channel_id=1, source_target_pairs={{0,1},{1,2},{2,3},{4,5},{5,6},{6,7},{8,9},{9,10},{10,11},{12,13},{... | collective-permute-start | bytes 1160 | tf_op jit(solution)/shard_map/while/body/eval_jaxpr/ppermute | solution.py:23
  361.1 5.0 %collective-permute-start.3 = (f32[3,1,32]{2,1,0:T(1,128)S(1)}, f32[3,1,32]{2,1,0:T(1,128)S(1)}, u32[]{:S(2)}, u32[]{:S(2)}) collective-permute-start(f32[3,1,32]{2,1,0:T(1,128)S(1)} %get-tuple-element.595), channel_id=1, source_target_pairs={{0,4},{4,8},{8,12},{12,16},{16,20},{20,24},{24,28},{1,5},{5,9},{9,... | collective-permute-start | bytes 1160 | tf_op jit(solution)/shard_map/while/body/eval_jaxpr/ppermute | solution.py:23
  377.7 5.2 %collective-permute-start.1 = (f32[3,1,32]{2,1,0:T(1,128)S(1)}, f32[3,1,32]{2,1,0:T(1,128)S(1)}, u32[]{:S(2)}, u32[]{:S(2)}) collective-permute-start(f32[3,1,32]{2,1,0:T(1,128)S(1)} %get-tuple-element.593), channel_id=1, source_target_pairs={{0,1},{1,2},{2,3},{4,5},{5,6},{6,7},{8,9},{9,10},{10,11},{12,13},{... | collective-permute-start | bytes 1160 | tf_op jit(solution)/shard_map/while/body/eval_jaxpr/ppermute | solution.py:23
  384.2 5.0 %collective-permute-start.3 = (f32[3,1,32]{2,1,0:T(1,128)S(1)}, f32[3,1,32]{2,1,0:T(1,128)S(1)}, u32[]{:S(2)}, u32[]{:S(2)}) collective-permute-start(f32[3,1,32]{2,1,0:T(1,128)S(1)} %get-tuple-element.595), channel_id=1, source_target_pairs={{0,4},{4,8},{8,12},{12,16},{16,20},{20,24},{24,28},{1,5},{5,9},{9,... | collective-permute-start | bytes 1160 | tf_op jit(solution)/shard_map/while/body/eval_jaxpr/ppermute | solution.py:23
  395.4 4.2 copy.25
  399.6 16.9 %gather_fusion.2 = bf16[2048,16,6]{1,2,0:T(8,128)(2,1)} fusion(bf16[16,6,2048]{0,1,2:T(8,128)(2,1)} %copy.25, s32[2048]{0:T(1024)S(1)} %fusion.34), kind=kCustom, calls=%fused_computation.2 | custom fusion | bytes 794624 | tf_op jit(solution)/shard_map/jit(_take)/gather | solution.py:162
  416.5 10.9 %fusion.43 = bf16[2048,6,16]{2,1,0:T(8,128)(2,1)} fusion(bf16[2048,16,6]{1,2,0:T(8,128)(2,1)} %gather_fusion.2, pred[2048]{0:T(1024)(128)(4,1)S(1)} %compare_and_fusion.1), kind=kLoop, calls=%fused_computation.91 | loop fusion | flops 196608 | bytes 788480
  427.4 5.0 %reshape.572 = bf16[4,2,24576]{2,1,0:T(2,128)(2,1)S(1)} reshape(bf16[2048,6,16]{2,1,0:T(8,128)(2,1)} %fusion.43) | data formatting | bytes 786432
  432.5 10.4 %all_to_all.5 = bf16[4,2,24576]{2,1,0:T(2,128)(2,1)S(1)} all-to-all(bf16[4,2,24576]{2,1,0:T(2,128)(2,1)S(1)} %reshape.572), channel_id=1, replica_groups=mesh['grp'=8,'dom'=4] {'dom'}, dimensions={0} | all-to-all | bytes 786432 | tf_op jit(solution)/shard_map/all_to_all | solution.py:163
  442.9 4.8 %reshape.573 = bf16[2048,6,16]{2,1,0:T(8,128)(2,1)} reshape(bf16[4,2,24576]{2,1,0:T(2,128)(2,1)S(1)} %all_to_all.5) | data formatting | bytes 786432
  447.7 4.9 %copy.26 = bf16[16,6,2048]{2,0,1:T(8,128)(2,1)} copy(bf16[16,6,2048]{0,1,2:T(8,128)(2,1)} %bitcast.204) | data formatting | bytes 786432 | tf_op jit(solution)/shard_map/all_to_all | solution.py:163
  (888 shorter events, 197.5 us)
Async XLA Ops:
  6.1 20.1 %collective-permute-start.4 = (f32[1,1,32]{2,1,0:T(1,128)S(1)}, f32[1,1,32]{2,1,0:T(1,128)S(1)}, u32[]{:S(2)}, u32[]{:S(2)}) collective-permute-start(f32[1,1,32]{2,1,0:T(1,128)S(1)} %get-tuple-element.361), channel_id=1, source_target_pairs={{0,4},{4,8},{8,12},{12,16},{16,20},{20,24},{24,28},{1,5},{5,9},{9,... | collective-permute-start | bytes 392 | tf_op jit(solution)/shard_map/ppermute | solution.py:23
  8.5 17.7 %collective-permute-start.7 = (f32[1,1,32]{2,1,0:T(1,128)S(1)}, f32[1,1,32]{2,1,0:T(1,128)S(1)}, u32[]{:S(2)}, u32[]{:S(2)}) collective-permute-start(f32[1,1,32]{2,1,0:T(1,128)S(1)} %get-tuple-element.362), channel_id=1, source_target_pairs={{1,0},{2,1},{3,2},{5,4},{6,5},{7,6},{9,8},{10,9},{11,10},{13,12},{... | collective-permute-start | bytes 392 | tf_op jit(solution)/shard_map/ppermute | solution.py:25
  9.8 16.4 %collective-permute-start.6 = (f32[1,1,32]{2,1,0:T(1,128)S(1)}, f32[1,1,32]{2,1,0:T(1,128)S(1)}, u32[]{:S(2)}, u32[]{:S(2)}) collective-permute-start(f32[1,1,32]{2,1,0:T(1,128)S(1)} %get-tuple-element.363), channel_id=1, source_target_pairs={{0,1},{1,2},{2,3},{4,5},{5,6},{6,7},{8,9},{9,10},{10,11},{12,13},{... | collective-permute-start | bytes 392 | tf_op jit(solution)/shard_map/ppermute | solution.py:23
  14.7 11.5 %collective-permute-start.5 = (f32[1,1,32]{2,1,0:T(1,128)S(1)}, f32[1,1,32]{2,1,0:T(1,128)S(1)}, u32[]{:S(2)}, u32[]{:S(2)}) collective-permute-start(f32[1,1,32]{2,1,0:T(1,128)S(1)} %get-tuple-element.364), channel_id=1, source_target_pairs={{4,0},{8,4},{12,8},{16,12},{20,16},{24,20},{28,24},{5,1},{9,5},{13... | collective-permute-start | bytes 392 | tf_op jit(solution)/shard_map/ppermute | solution.py:25
  32.0 12.3 %collective-permute-start = (f32[3,1,32]{2,1,0:T(1,128)S(1)}, f32[3,1,32]{2,1,0:T(1,128)S(1)}, u32[]{:S(2)}, u32[]{:S(2)}) collective-permute-start(f32[3,1,32]{2,1,0:T(1,128)S(1)} %get-tuple-element.592), channel_id=1, source_target_pairs={{1,0},{2,1},{3,2},{5,4},{6,5},{7,6},{9,8},{10,9},{11,10},{13,12},{... | collective-permute-start | bytes 1160 | tf_op jit(solution)/shard_map/while/body/eval_jaxpr/ppermute | solution.py:25
  33.3 11.0 %collective-permute-start.1 = (f32[3,1,32]{2,1,0:T(1,128)S(1)}, f32[3,1,32]{2,1,0:T(1,128)S(1)}, u32[]{:S(2)}, u32[]{:S(2)}) collective-permute-start(f32[3,1,32]{2,1,0:T(1,128)S(1)} %get-tuple-element.593), channel_id=1, source_target_pairs={{0,1},{1,2},{2,3},{4,5},{5,6},{6,7},{8,9},{9,10},{10,11},{12,13},{... | collective-permute-start | bytes 1160 | tf_op jit(solution)/shard_map/while/body/eval_jaxpr/ppermute | solution.py:23
  54.5 12.3 %collective-permute-start = (f32[3,1,32]{2,1,0:T(1,128)S(1)}, f32[3,1,32]{2,1,0:T(1,128)S(1)}, u32[]{:S(2)}, u32[]{:S(2)}) collective-permute-start(f32[3,1,32]{2,1,0:T(1,128)S(1)} %get-tuple-element.592), channel_id=1, source_target_pairs={{1,0},{2,1},{3,2},{5,4},{6,5},{7,6},{9,8},{10,9},{11,10},{13,12},{... | collective-permute-start | bytes 1160 | tf_op jit(solution)/shard_map/while/body/eval_jaxpr/ppermute | solution.py:25
  55.8 11.0 %collective-permute-start.1 = (f32[3,1,32]{2,1,0:T(1,128)S(1)}, f32[3,1,32]{2,1,0:T(1,128)S(1)}, u32[]{:S(2)}, u32[]{:S(2)}) collective-permute-start(f32[3,1,32]{2,1,0:T(1,128)S(1)} %get-tuple-element.593), channel_id=1, source_target_pairs={{0,1},{1,2},{2,3},{4,5},{5,6},{6,7},{8,9},{9,10},{10,11},{12,13},{... | collective-permute-start | bytes 1160 | tf_op jit(solution)/shard_map/while/body/eval_jaxpr/ppermute | solution.py:23
  77.0 12.8 %collective-permute-start = (f32[3,1,32]{2,1,0:T(1,128)S(1)}, f32[3,1,32]{2,1,0:T(1,128)S(1)}, u32[]{:S(2)}, u32[]{:S(2)}) collective-permute-start(f32[3,1,32]{2,1,0:T(1,128)S(1)} %get-tuple-element.592), channel_id=1, source_target_pairs={{1,0},{2,1},{3,2},{5,4},{6,5},{7,6},{9,8},{10,9},{11,10},{13,12},{... | collective-permute-start | bytes 1160 | tf_op jit(solution)/shard_map/while/body/eval_jaxpr/ppermute | solution.py:25
  78.2 11.5 %collective-permute-start.1 = (f32[3,1,32]{2,1,0:T(1,128)S(1)}, f32[3,1,32]{2,1,0:T(1,128)S(1)}, u32[]{:S(2)}, u32[]{:S(2)}) collective-permute-start(f32[3,1,32]{2,1,0:T(1,128)S(1)} %get-tuple-element.593), channel_id=1, source_target_pairs={{0,1},{1,2},{2,3},{4,5},{5,6},{6,7},{8,9},{9,10},{10,11},{12,13},{... | collective-permute-start | bytes 1160 | tf_op jit(solution)/shard_map/while/body/eval_jaxpr/ppermute | solution.py:23
  83.4 6.4 %collective-permute-start.2 = (f32[3,1,32]{2,1,0:T(1,128)S(1)}, f32[3,1,32]{2,1,0:T(1,128)S(1)}, u32[]{:S(2)}, u32[]{:S(2)}) collective-permute-start(f32[3,1,32]{2,1,0:T(1,128)S(1)} %get-tuple-element.594), channel_id=1, source_target_pairs={{4,0},{8,4},{12,8},{16,12},{20,16},{24,20},{28,24},{5,1},{9,5},{13... | collective-permute-start | bytes 1160 | tf_op jit(solution)/shard_map/while/body/eval_jaxpr/ppermute | solution.py:25
  100.0 12.8 %collective-permute-start = (f32[3,1,32]{2,1,0:T(1,128)S(1)}, f32[3,1,32]{2,1,0:T(1,128)S(1)}, u32[]{:S(2)}, u32[]{:S(2)}) collective-permute-start(f32[3,1,32]{2,1,0:T(1,128)S(1)} %get-tuple-element.592), channel_id=1, source_target_pairs={{1,0},{2,1},{3,2},{5,4},{6,5},{7,6},{9,8},{10,9},{11,10},{13,12},{... | collective-permute-start | bytes 1160 | tf_op jit(solution)/shard_map/while/body/eval_jaxpr/ppermute | solution.py:25
  101.3 11.5 %collective-permute-start.1 = (f32[3,1,32]{2,1,0:T(1,128)S(1)}, f32[3,1,32]{2,1,0:T(1,128)S(1)}, u32[]{:S(2)}, u32[]{:S(2)}) collective-permute-start(f32[3,1,32]{2,1,0:T(1,128)S(1)} %get-tuple-element.593), channel_id=1, source_target_pairs={{0,1},{1,2},{2,3},{4,5},{5,6},{6,7},{8,9},{9,10},{10,11},{12,13},{... | collective-permute-start | bytes 1160 | tf_op jit(solution)/shard_map/while/body/eval_jaxpr/ppermute | solution.py:23
  106.5 6.4 %collective-permute-start.2 = (f32[3,1,32]{2,1,0:T(1,128)S(1)}, f32[3,1,32]{2,1,0:T(1,128)S(1)}, u32[]{:S(2)}, u32[]{:S(2)}) collective-permute-start(f32[3,1,32]{2,1,0:T(1,128)S(1)} %get-tuple-element.594), channel_id=1, source_target_pairs={{4,0},{8,4},{12,8},{16,12},{20,16},{24,20},{28,24},{5,1},{9,5},{13... | collective-permute-start | bytes 1160 | tf_op jit(solution)/shard_map/while/body/eval_jaxpr/ppermute | solution.py:25
  123.0 12.8 %collective-permute-start = (f32[3,1,32]{2,1,0:T(1,128)S(1)}, f32[3,1,32]{2,1,0:T(1,128)S(1)}, u32[]{:S(2)}, u32[]{:S(2)}) collective-permute-start(f32[3,1,32]{2,1,0:T(1,128)S(1)} %get-tuple-element.592), channel_id=1, source_target_pairs={{1,0},{2,1},{3,2},{5,4},{6,5},{7,6},{9,8},{10,9},{11,10},{13,12},{... | collective-permute-start | bytes 1160 | tf_op jit(solution)/shard_map/while/body/eval_jaxpr/ppermute | solution.py:25
  124.3 11.5 %collective-permute-start.1 = (f32[3,1,32]{2,1,0:T(1,128)S(1)}, f32[3,1,32]{2,1,0:T(1,128)S(1)}, u32[]{:S(2)}, u32[]{:S(2)}) collective-permute-start(f32[3,1,32]{2,1,0:T(1,128)S(1)} %get-tuple-element.593), channel_id=1, source_target_pairs={{0,1},{1,2},{2,3},{4,5},{5,6},{6,7},{8,9},{9,10},{10,11},{12,13},{... | collective-permute-start | bytes 1160 | tf_op jit(solution)/shard_map/while/body/eval_jaxpr/ppermute | solution.py:23
  146.1 12.8 %collective-permute-start = (f32[3,1,32]{2,1,0:T(1,128)S(1)}, f32[3,1,32]{2,1,0:T(1,128)S(1)}, u32[]{:S(2)}, u32[]{:S(2)}) collective-permute-start(f32[3,1,32]{2,1,0:T(1,128)S(1)} %get-tuple-element.592), channel_id=1, source_target_pairs={{1,0},{2,1},{3,2},{5,4},{6,5},{7,6},{9,8},{10,9},{11,10},{13,12},{... | collective-permute-start | bytes 1160 | tf_op jit(solution)/shard_map/while/body/eval_jaxpr/ppermute | solution.py:25
  147.4 11.5 %collective-permute-start.1 = (f32[3,1,32]{2,1,0:T(1,128)S(1)}, f32[3,1,32]{2,1,0:T(1,128)S(1)}, u32[]{:S(2)}, u32[]{:S(2)}) collective-permute-start(f32[3,1,32]{2,1,0:T(1,128)S(1)} %get-tuple-element.593), channel_id=1, source_target_pairs={{0,1},{1,2},{2,3},{4,5},{5,6},{6,7},{8,9},{9,10},{10,11},{12,13},{... | collective-permute-start | bytes 1160 | tf_op jit(solution)/shard_map/while/body/eval_jaxpr/ppermute | solution.py:23
  152.5 6.4 %collective-permute-start.2 = (f32[3,1,32]{2,1,0:T(1,128)S(1)}, f32[3,1,32]{2,1,0:T(1,128)S(1)}, u32[]{:S(2)}, u32[]{:S(2)}) collective-permute-start(f32[3,1,32]{2,1,0:T(1,128)S(1)} %get-tuple-element.594), channel_id=1, source_target_pairs={{4,0},{8,4},{12,8},{16,12},{20,16},{24,20},{28,24},{5,1},{9,5},{13... | collective-permute-start | bytes 1160 | tf_op jit(solution)/shard_map/while/body/eval_jaxpr/ppermute | solution.py:25
  169.1 12.8 %collective-permute-start = (f32[3,1,32]{2,1,0:T(1,128)S(1)}, f32[3,1,32]{2,1,0:T(1,128)S(1)}, u32[]{:S(2)}, u32[]{:S(2)}) collective-permute-start(f32[3,1,32]{2,1,0:T(1,128)S(1)} %get-tuple-element.592), channel_id=1, source_target_pairs={{1,0},{2,1},{3,2},{5,4},{6,5},{7,6},{9,8},{10,9},{11,10},{13,12},{... | collective-permute-start | bytes 1160 | tf_op jit(solution)/shard_map/while/body/eval_jaxpr/ppermute | solution.py:25
  170.4 11.5 %collective-permute-start.1 = (f32[3,1,32]{2,1,0:T(1,128)S(1)}, f32[3,1,32]{2,1,0:T(1,128)S(1)}, u32[]{:S(2)}, u32[]{:S(2)}) collective-permute-start(f32[3,1,32]{2,1,0:T(1,128)S(1)} %get-tuple-element.593), channel_id=1, source_target_pairs={{0,1},{1,2},{2,3},{4,5},{5,6},{6,7},{8,9},{9,10},{10,11},{12,13},{... | collective-permute-start | bytes 1160 | tf_op jit(solution)/shard_map/while/body/eval_jaxpr/ppermute | solution.py:23
  175.6 6.4 %collective-permute-start.2 = (f32[3,1,32]{2,1,0:T(1,128)S(1)}, f32[3,1,32]{2,1,0:T(1,128)S(1)}, u32[]{:S(2)}, u32[]{:S(2)}) collective-permute-start(f32[3,1,32]{2,1,0:T(1,128)S(1)} %get-tuple-element.594), channel_id=1, source_target_pairs={{4,0},{8,4},{12,8},{16,12},{20,16},{24,20},{28,24},{5,1},{9,5},{13... | collective-permute-start | bytes 1160 | tf_op jit(solution)/shard_map/while/body/eval_jaxpr/ppermute | solution.py:25
  192.1 12.8 %collective-permute-start = (f32[3,1,32]{2,1,0:T(1,128)S(1)}, f32[3,1,32]{2,1,0:T(1,128)S(1)}, u32[]{:S(2)}, u32[]{:S(2)}) collective-permute-start(f32[3,1,32]{2,1,0:T(1,128)S(1)} %get-tuple-element.592), channel_id=1, source_target_pairs={{1,0},{2,1},{3,2},{5,4},{6,5},{7,6},{9,8},{10,9},{11,10},{13,12},{... | collective-permute-start | bytes 1160 | tf_op jit(solution)/shard_map/while/body/eval_jaxpr/ppermute | solution.py:25
  193.4 11.5 %collective-permute-start.1 = (f32[3,1,32]{2,1,0:T(1,128)S(1)}, f32[3,1,32]{2,1,0:T(1,128)S(1)}, u32[]{:S(2)}, u32[]{:S(2)}) collective-permute-start(f32[3,1,32]{2,1,0:T(1,128)S(1)} %get-tuple-element.593), channel_id=1, source_target_pairs={{0,1},{1,2},{2,3},{4,5},{5,6},{6,7},{8,9},{9,10},{10,11},{12,13},{... | collective-permute-start | bytes 1160 | tf_op jit(solution)/shard_map/while/body/eval_jaxpr/ppermute | solution.py:23
  198.6 6.4 %collective-permute-start.2 = (f32[3,1,32]{2,1,0:T(1,128)S(1)}, f32[3,1,32]{2,1,0:T(1,128)S(1)}, u32[]{:S(2)}, u32[]{:S(2)}) collective-permute-start(f32[3,1,32]{2,1,0:T(1,128)S(1)} %get-tuple-element.594), channel_id=1, source_target_pairs={{4,0},{8,4},{12,8},{16,12},{20,16},{24,20},{28,24},{5,1},{9,5},{13... | collective-permute-start | bytes 1160 | tf_op jit(solution)/shard_map/while/body/eval_jaxpr/ppermute | solution.py:25
  215.2 12.8 %collective-permute-start = (f32[3,1,32]{2,1,0:T(1,128)S(1)}, f32[3,1,32]{2,1,0:T(1,128)S(1)}, u32[]{:S(2)}, u32[]{:S(2)}) collective-permute-start(f32[3,1,32]{2,1,0:T(1,128)S(1)} %get-tuple-element.592), channel_id=1, source_target_pairs={{1,0},{2,1},{3,2},{5,4},{6,5},{7,6},{9,8},{10,9},{11,10},{13,12},{... | collective-permute-start | bytes 1160 | tf_op jit(solution)/shard_map/while/body/eval_jaxpr/ppermute | solution.py:25
  216.5 11.5 %collective-permute-start.1 = (f32[3,1,32]{2,1,0:T(1,128)S(1)}, f32[3,1,32]{2,1,0:T(1,128)S(1)}, u32[]{:S(2)}, u32[]{:S(2)}) collective-permute-start(f32[3,1,32]{2,1,0:T(1,128)S(1)} %get-tuple-element.593), channel_id=1, source_target_pairs={{0,1},{1,2},{2,3},{4,5},{5,6},{6,7},{8,9},{9,10},{10,11},{12,13},{... | collective-permute-start | bytes 1160 | tf_op jit(solution)/shard_map/while/body/eval_jaxpr/ppermute | solution.py:23
  221.6 6.4 %collective-permute-start.2 = (f32[3,1,32]{2,1,0:T(1,128)S(1)}, f32[3,1,32]{2,1,0:T(1,128)S(1)}, u32[]{:S(2)}, u32[]{:S(2)}) collective-permute-start(f32[3,1,32]{2,1,0:T(1,128)S(1)} %get-tuple-element.594), channel_id=1, source_target_pairs={{4,0},{8,4},{12,8},{16,12},{20,16},{24,20},{28,24},{5,1},{9,5},{13... | collective-permute-start | bytes 1160 | tf_op jit(solution)/shard_map/while/body/eval_jaxpr/ppermute | solution.py:25
  238.2 12.8 %collective-permute-start = (f32[3,1,32]{2,1,0:T(1,128)S(1)}, f32[3,1,32]{2,1,0:T(1,128)S(1)}, u32[]{:S(2)}, u32[]{:S(2)}) collective-permute-start(f32[3,1,32]{2,1,0:T(1,128)S(1)} %get-tuple-element.592), channel_id=1, source_target_pairs={{1,0},{2,1},{3,2},{5,4},{6,5},{7,6},{9,8},{10,9},{11,10},{13,12},{... | collective-permute-start | bytes 1160 | tf_op jit(solution)/shard_map/while/body/eval_jaxpr/ppermute | solution.py:25
  239.5 11.5 %collective-permute-start.1 = (f32[3,1,32]{2,1,0:T(1,128)S(1)}, f32[3,1,32]{2,1,0:T(1,128)S(1)}, u32[]{:S(2)}, u32[]{:S(2)}) collective-permute-start(f32[3,1,32]{2,1,0:T(1,128)S(1)} %get-tuple-element.593), channel_id=1, source_target_pairs={{0,1},{1,2},{2,3},{4,5},{5,6},{6,7},{8,9},{9,10},{10,11},{12,13},{... | collective-permute-start | bytes 1160 | tf_op jit(solution)/shard_map/while/body/eval_jaxpr/ppermute | solution.py:23
  244.7 6.4 %collective-permute-start.2 = (f32[3,1,32]{2,1,0:T(1,128)S(1)}, f32[3,1,32]{2,1,0:T(1,128)S(1)}, u32[]{:S(2)}, u32[]{:S(2)}) collective-permute-start(f32[3,1,32]{2,1,0:T(1,128)S(1)} %get-tuple-element.594), channel_id=1, source_target_pairs={{4,0},{8,4},{12,8},{16,12},{20,16},{24,20},{28,24},{5,1},{9,5},{13... | collective-permute-start | bytes 1160 | tf_op jit(solution)/shard_map/while/body/eval_jaxpr/ppermute | solution.py:25
  261.2 12.8 %collective-permute-start = (f32[3,1,32]{2,1,0:T(1,128)S(1)}, f32[3,1,32]{2,1,0:T(1,128)S(1)}, u32[]{:S(2)}, u32[]{:S(2)}) collective-permute-start(f32[3,1,32]{2,1,0:T(1,128)S(1)} %get-tuple-element.592), channel_id=1, source_target_pairs={{1,0},{2,1},{3,2},{5,4},{6,5},{7,6},{9,8},{10,9},{11,10},{13,12},{... | collective-permute-start | bytes 1160 | tf_op jit(solution)/shard_map/while/body/eval_jaxpr/ppermute | solution.py:25
  262.5 11.5 %collective-permute-start.1 = (f32[3,1,32]{2,1,0:T(1,128)S(1)}, f32[3,1,32]{2,1,0:T(1,128)S(1)}, u32[]{:S(2)}, u32[]{:S(2)}) collective-permute-start(f32[3,1,32]{2,1,0:T(1,128)S(1)} %get-tuple-element.593), channel_id=1, source_target_pairs={{0,1},{1,2},{2,3},{4,5},{5,6},{6,7},{8,9},{9,10},{10,11},{12,13},{... | collective-permute-start | bytes 1160 | tf_op jit(solution)/shard_map/while/body/eval_jaxpr/ppermute | solution.py:23
  267.7 6.4 %collective-permute-start.2 = (f32[3,1,32]{2,1,0:T(1,128)S(1)}, f32[3,1,32]{2,1,0:T(1,128)S(1)}, u32[]{:S(2)}, u32[]{:S(2)}) collective-permute-start(f32[3,1,32]{2,1,0:T(1,128)S(1)} %get-tuple-element.594), channel_id=1, source_target_pairs={{4,0},{8,4},{12,8},{16,12},{20,16},{24,20},{28,24},{5,1},{9,5},{13... | collective-permute-start | bytes 1160 | tf_op jit(solution)/shard_map/while/body/eval_jaxpr/ppermute | solution.py:25
  284.3 12.8 %collective-permute-start = (f32[3,1,32]{2,1,0:T(1,128)S(1)}, f32[3,1,32]{2,1,0:T(1,128)S(1)}, u32[]{:S(2)}, u32[]{:S(2)}) collective-permute-start(f32[3,1,32]{2,1,0:T(1,128)S(1)} %get-tuple-element.592), channel_id=1, source_target_pairs={{1,0},{2,1},{3,2},{5,4},{6,5},{7,6},{9,8},{10,9},{11,10},{13,12},{... | collective-permute-start | bytes 1160 | tf_op jit(solution)/shard_map/while/body/eval_jaxpr/ppermute | solution.py:25
  285.6 11.5 %collective-permute-start.1 = (f32[3,1,32]{2,1,0:T(1,128)S(1)}, f32[3,1,32]{2,1,0:T(1,128)S(1)}, u32[]{:S(2)}, u32[]{:S(2)}) collective-permute-start(f32[3,1,32]{2,1,0:T(1,128)S(1)} %get-tuple-element.593), channel_id=1, source_target_pairs={{0,1},{1,2},{2,3},{4,5},{5,6},{6,7},{8,9},{9,10},{10,11},{12,13},{... | collective-permute-start | bytes 1160 | tf_op jit(solution)/shard_map/while/body/eval_jaxpr/ppermute | solution.py:23
  307.3 12.8 %collective-permute-start = (f32[3,1,32]{2,1,0:T(1,128)S(1)}, f32[3,1,32]{2,1,0:T(1,128)S(1)}, u32[]{:S(2)}, u32[]{:S(2)}) collective-permute-start(f32[3,1,32]{2,1,0:T(1,128)S(1)} %get-tuple-element.592), channel_id=1, source_target_pairs={{1,0},{2,1},{3,2},{5,4},{6,5},{7,6},{9,8},{10,9},{11,10},{13,12},{... | collective-permute-start | bytes 1160 | tf_op jit(solution)/shard_map/while/body/eval_jaxpr/ppermute | solution.py:25
  308.6 11.5 %collective-permute-start.1 = (f32[3,1,32]{2,1,0:T(1,128)S(1)}, f32[3,1,32]{2,1,0:T(1,128)S(1)}, u32[]{:S(2)}, u32[]{:S(2)}) collective-permute-start(f32[3,1,32]{2,1,0:T(1,128)S(1)} %get-tuple-element.593), channel_id=1, source_target_pairs={{0,1},{1,2},{2,3},{4,5},{5,6},{6,7},{8,9},{9,10},{10,11},{12,13},{... | collective-permute-start | bytes 1160 | tf_op jit(solution)/shard_map/while/body/eval_jaxpr/ppermute | solution.py:23
  313.8 6.4 %collective-permute-start.2 = (f32[3,1,32]{2,1,0:T(1,128)S(1)}, f32[3,1,32]{2,1,0:T(1,128)S(1)}, u32[]{:S(2)}, u32[]{:S(2)}) collective-permute-start(f32[3,1,32]{2,1,0:T(1,128)S(1)} %get-tuple-element.594), channel_id=1, source_target_pairs={{4,0},{8,4},{12,8},{16,12},{20,16},{24,20},{28,24},{5,1},{9,5},{13... | collective-permute-start | bytes 1160 | tf_op jit(solution)/shard_map/while/body/eval_jaxpr/ppermute | solution.py:25
  330.3 12.8 %collective-permute-start = (f32[3,1,32]{2,1,0:T(1,128)S(1)}, f32[3,1,32]{2,1,0:T(1,128)S(1)}, u32[]{:S(2)}, u32[]{:S(2)}) collective-permute-start(f32[3,1,32]{2,1,0:T(1,128)S(1)} %get-tuple-element.592), channel_id=1, source_target_pairs={{1,0},{2,1},{3,2},{5,4},{6,5},{7,6},{9,8},{10,9},{11,10},{13,12},{... | collective-permute-start | bytes 1160 | tf_op jit(solution)/shard_map/while/body/eval_jaxpr/ppermute | solution.py:25
  331.6 11.5 %collective-permute-start.1 = (f32[3,1,32]{2,1,0:T(1,128)S(1)}, f32[3,1,32]{2,1,0:T(1,128)S(1)}, u32[]{:S(2)}, u32[]{:S(2)}) collective-permute-start(f32[3,1,32]{2,1,0:T(1,128)S(1)} %get-tuple-element.593), channel_id=1, source_target_pairs={{0,1},{1,2},{2,3},{4,5},{5,6},{6,7},{8,9},{9,10},{10,11},{12,13},{... | collective-permute-start | bytes 1160 | tf_op jit(solution)/shard_map/while/body/eval_jaxpr/ppermute | solution.py:23
  336.8 6.4 %collective-permute-start.2 = (f32[3,1,32]{2,1,0:T(1,128)S(1)}, f32[3,1,32]{2,1,0:T(1,128)S(1)}, u32[]{:S(2)}, u32[]{:S(2)}) collective-permute-start(f32[3,1,32]{2,1,0:T(1,128)S(1)} %get-tuple-element.594), channel_id=1, source_target_pairs={{4,0},{8,4},{12,8},{16,12},{20,16},{24,20},{28,24},{5,1},{9,5},{13... | collective-permute-start | bytes 1160 | tf_op jit(solution)/shard_map/while/body/eval_jaxpr/ppermute | solution.py:25
  353.4 12.8 %collective-permute-start = (f32[3,1,32]{2,1,0:T(1,128)S(1)}, f32[3,1,32]{2,1,0:T(1,128)S(1)}, u32[]{:S(2)}, u32[]{:S(2)}) collective-permute-start(f32[3,1,32]{2,1,0:T(1,128)S(1)} %get-tuple-element.592), channel_id=1, source_target_pairs={{1,0},{2,1},{3,2},{5,4},{6,5},{7,6},{9,8},{10,9},{11,10},{13,12},{... | collective-permute-start | bytes 1160 | tf_op jit(solution)/shard_map/while/body/eval_jaxpr/ppermute | solution.py:25
  354.7 11.5 %collective-permute-start.1 = (f32[3,1,32]{2,1,0:T(1,128)S(1)}, f32[3,1,32]{2,1,0:T(1,128)S(1)}, u32[]{:S(2)}, u32[]{:S(2)}) collective-permute-start(f32[3,1,32]{2,1,0:T(1,128)S(1)} %get-tuple-element.593), channel_id=1, source_target_pairs={{0,1},{1,2},{2,3},{4,5},{5,6},{6,7},{8,9},{9,10},{10,11},{12,13},{... | collective-permute-start | bytes 1160 | tf_op jit(solution)/shard_map/while/body/eval_jaxpr/ppermute | solution.py:23
  359.8 6.4 %collective-permute-start.2 = (f32[3,1,32]{2,1,0:T(1,128)S(1)}, f32[3,1,32]{2,1,0:T(1,128)S(1)}, u32[]{:S(2)}, u32[]{:S(2)}) collective-permute-start(f32[3,1,32]{2,1,0:T(1,128)S(1)} %get-tuple-element.594), channel_id=1, source_target_pairs={{4,0},{8,4},{12,8},{16,12},{20,16},{24,20},{28,24},{5,1},{9,5},{13... | collective-permute-start | bytes 1160 | tf_op jit(solution)/shard_map/while/body/eval_jaxpr/ppermute | solution.py:25
  376.4 12.8 %collective-permute-start = (f32[3,1,32]{2,1,0:T(1,128)S(1)}, f32[3,1,32]{2,1,0:T(1,128)S(1)}, u32[]{:S(2)}, u32[]{:S(2)}) collective-permute-start(f32[3,1,32]{2,1,0:T(1,128)S(1)} %get-tuple-element.592), channel_id=1, source_target_pairs={{1,0},{2,1},{3,2},{5,4},{6,5},{7,6},{9,8},{10,9},{11,10},{13,12},{... | collective-permute-start | bytes 1160 | tf_op jit(solution)/shard_map/while/body/eval_jaxpr/ppermute | solution.py:25
  377.7 11.5 %collective-permute-start.1 = (f32[3,1,32]{2,1,0:T(1,128)S(1)}, f32[3,1,32]{2,1,0:T(1,128)S(1)}, u32[]{:S(2)}, u32[]{:S(2)}) collective-permute-start(f32[3,1,32]{2,1,0:T(1,128)S(1)} %get-tuple-element.593), channel_id=1, source_target_pairs={{0,1},{1,2},{2,3},{4,5},{5,6},{6,7},{8,9},{9,10},{10,11},{12,13},{... | collective-permute-start | bytes 1160 | tf_op jit(solution)/shard_map/while/body/eval_jaxpr/ppermute | solution.py:23
  382.9 6.4 %collective-permute-start.2 = (f32[3,1,32]{2,1,0:T(1,128)S(1)}, f32[3,1,32]{2,1,0:T(1,128)S(1)}, u32[]{:S(2)}, u32[]{:S(2)}) collective-permute-start(f32[3,1,32]{2,1,0:T(1,128)S(1)} %get-tuple-element.594), channel_id=1, source_target_pairs={{4,0},{8,4},{12,8},{16,12},{20,16},{24,20},{28,24},{5,1},{9,5},{13... | collective-permute-start | bytes 1160 | tf_op jit(solution)/shard_map/while/body/eval_jaxpr/ppermute | solution.py:25
  (28 other events, 338.3 us)
where the time goes:
time: 459 us; the launch traced here: 453 us
  starting transfers between devices  213 us (46%)
  matrix products  90.2 us (20%)
  local copies, waits for them, and re-layouts  77.7 us (17%)
  other arithmetic  44.4 us (10%)
  waiting for transfers between devices  12.1 us (3%)
  blocking collectives  10.4 us (2%)
  loops' own time  4.88 us (1%)
    ppermute x34, starting transfers between devices, extended(): lax.ppermute(tail, axis, [(i, (i + 1) % count) for i in range(ends)])  169 us
    dot_general x16, matrix products, gather_nodes(): lax.dot_general(displace, incidence.astype(jnp.float32), (((1,), (1,)), (...  48.8 us
    ppermute x34, starting transfers between devices, extended(): lax.ppermute(head, axis, [((i + 1) % count, i) for i in range(ends)])  43.9 us
    dot_general x17, matrix products, scatter_nodes(): jnp.dot(flat, incidence.astype(jnp.float32), precision=lax.Precision.HIGH...  34.2 us
    scatter-add x17, other arithmetic, assemble(): node_field.at[:, shared_nodes].add(received * neighbour_mask[None, :, None])  23.2 us
    gather x1, local copies, waits for them, and re-layouts, shards(): ordered = jnp.take(strain_store, inverse_rank, axis=2)  16.9 us
    gather x34, local copies, waits for them, and re-layouts, assemble(): picked = jnp.take(node_field, shared_nodes, axis=1)  13.2 us
    ppermute x34, waiting for transfers between devices, extended(): lax.ppermute(tail, axis, [(i, (i + 1) % count) for i in range(ends)])  12 us
  transfers between devices with their start and end apart: 68, of which 16 were waited for; matrix products, arithmetic and copies ran while one was open for 2% of the time, Pallas kernels for 0%

commit v1 on v0

v1 whole, which is shorter than its diff:
```python
import functools

import jax
import jax.numpy as jnp
from jax import lax
from jax.experimental import pallas as pl
from jax.experimental.pallas import tpu as pltpu
from jax.sharding import PartitionSpec as P

MESH = pl.DeviceIdType.MESH
F32 = jnp.float32
BF16 = jnp.bfloat16
time_step = 0.5
LANES = 128


def split(x):
    hi = x.astype(BF16)
    return hi, (x - hi.astype(F32)).astype(BF16)


def pick_lanes(x, idx):
    return jnp.take_along_axis(x, idx, axis=1, mode="promise_in_bounds")


def kernel(
    groups,
    writers,
    steps,
    nodes_el,
    conn_ref,
    connt_ref,
    facet_ref,
    facesw_ref,
    nb_ref,
    rankt_ref,
    w1f_ref,
    w2f_ref,
    jac_ref,
    lame_ref,
    pw_ref,
    mass_ref,
    src_ref,
    wav_ref,
    out_ref,
    onehot,
    hmask,
    perm,
    w1,
    w2,
    snaps,
    lhs,
    ordered,
    send,
    recv,
    send_sem,
    recv_sem,
    out_send_sem,
    out_recv_sem,
):
    g = lax.axis_index("grp")
    d = lax.axis_index("dom")
    points = pw_ref.shape[0]
    block = out_ref.shape[2] // writers
    blocks = src_ref.shape[1] // LANES

    recv[...] = jnp.zeros_like(recv)
    has = (g > 0, g < groups - 1, d > 0, d < writers - 1)
    where_to = ((g - 1, d), (g + 1, d), (g, d - 1), (g, d + 1))

    barrier = pltpu.get_barrier_semaphore()
    for k in range(2):

        @pl.when(has[k])
        def _():
            pl.semaphore_signal(barrier, inc=1, device_id=where_to[k], device_id_type=MESH)

    for i in range(1, writers):
        pl.semaphore_signal(
            barrier, inc=1, device_id=(g, lax.rem(d + i, writers)), device_id_type=MESH
        )

    lane128 = lax.broadcasted_iota(jnp.int32, (LANES, LANES), 1)
    row16 = lax.broadcasted_iota(jnp.int32, (16, LANES), 0)
    for n in range(nodes_el):
        low = jnp.bitwise_and(connt_ref[:, n : n + 1], LANES - 1)
        onehot[n * LANES : (n + 1) * LANES, :] = jnp.where(low == lane128, 1.0, 0.0).astype(BF16)
        high = jnp.right_shift(conn_ref[n : n + 1, :], 7)
        hmask[n * 16 : (n + 1) * 16, :] = jnp.where(
            high == jnp.right_shift(row16, 2), 1.0, 0.0
        ).astype(BF16)
    for ref, full in ((w1, w1f_ref), (w2, w2f_ref)):
        hi, lo = split(full[...])
        col = lax.broadcasted_iota(jnp.int32, full.shape, 1)
        ref[...] = jnp.where(
            col < (full.shape[1] // 3) * 2, hi.astype(F32), lo.astype(F32)
        ).astype(BF16)

    facesw = facesw_ref[...]
    face_low = jnp.broadcast_to(jnp.bitwise_and(facesw, LANES - 1), (8, LANES))
    face_mask = jnp.where(
        jnp.right_shift(facesw, 7) == jnp.right_shift(row16, 2), 1.0, 0.0
    )
    position = lax.broadcasted_iota(jnp.int32, (LANES, LANES), 0).astype(F32)
    inv_rows = []
    has_rows = []
    for b in range(blocks):
        hit = jnp.where(facet_ref[...] == lane128 + b * LANES, 1.0, 0.0)
        inv_rows.append(
            jnp.broadcast_to(jnp.sum(hit * position, axis=0, keepdims=True), (4, LANES))
        )
        has_rows.append(jnp.broadcast_to(jnp.sum(hit, axis=0, keepdims=True), (4, LANES)))
    inv_idx = jnp.concatenate(inv_rows, axis=0).astype(jnp.int32)
    inv_has = jnp.concatenate(has_rows, axis=0)
    quarter = jnp.right_shift(lax.broadcasted_iota(jnp.int32, (8, LANES), 1), 5)
    nb = nb_ref[...].astype(F32)
    recv_mask = [jnp.where(quarter == k, nb[:, k : k + 1], 0.0) for k in range(4)]

    def copies(slot):
        return [
            pltpu.make_async_remote_copy(
                src_ref=send.at[slot],
                dst_ref=recv.at[slot, k ^ 1],
                send_sem=send_sem.at[slot, k],
                recv_sem=recv_sem.at[slot, k ^ 1],
                device_id=where_to[k],
                device_id_type=MESH,
            )
            for k in range(4)
        ]

    def arrivals(slot):
        return [
            pltpu.make_async_remote_copy(
                src_ref=send.at[slot],
                dst_ref=recv.at[slot, k],
                send_sem=send_sem.at[slot, k],
                recv_sem=recv_sem.at[slot, k],
                device_id=where_to[k],
                device_id_type=MESH,
            )
            for k in range(4)
        ]

    def send_shared(field, slot):
        part = pick_lanes(field[0:8], face_low) * face_mask[0:8]
        part = part + pick_lanes(field[8:16], face_low) * face_mask[8:16]
        send[slot] = part + pltpu.roll(part, 4, 0)
        for k, copy in enumerate(copies(slot)):

            @pl.when(has[k])
            def _():
                copy.start()

    def add_shared(field, slot):
        for k, copy in enumerate(arrivals(slot)):

            @pl.when(has[k])
            def _():
                copy.wait_recv()
                copy.wait_send()

        got = recv[slot, 0] * recv_mask[0]
        for k in range(1, 4):
            got = got + recv[slot, k] * recv_mask[k]
        added = jnp.concatenate(
            [pick_lanes(got, inv_idx[0:8]), pick_lanes(got, inv_idx[8:16])], axis=0
        )
        return field + added * inv_has

    def scatter(rows):
        pieces = []
        for n in range(nodes_el):
            v = rows(n)
            hi, lo = split(jnp.concatenate([v, v], axis=0))
            mask = hmask[n * 16 : (n + 1) * 16, :]
            pieces.append(jnp.concatenate([hi * mask, lo * mask], axis=0))
        res = jnp.dot(
            jnp.concatenate(pieces, axis=1), onehot[...], preferred_element_type=F32
        )
        return res[0:16] + res[16:32]

    row8 = lax.broadcasted_iota(jnp.int32, (8, LANES), 0)
    mass_row = jnp.bitwise_and(row8, 3) == 3
    mass = scatter(lambda n: jnp.where(mass_row, mass_ref[n : n + 1, :], 0.0))
    src_rows = []
    for b in range(blocks):
        src_rows.append(src_ref[:, b * LANES : (b + 1) * LANES])
        src_rows.append(jnp.zeros((1, LANES), F32))
    first = mass + jnp.concatenate(src_rows, axis=0)

    pl.semaphore_wait(
        barrier, has[0].astype(jnp.int32) + has[1].astype(jnp.int32) + writers - 1
    )
    send_shared(first, 0)

    lane_perm = lax.broadcasted_iota(jnp.int32, (LANES, LANES), 1)
    for q in range(points):
        column = rankt_ref[:, q : q + 1]

        def build(j, carry):
            start = pl.multiple_of(j * LANES, LANES)
            perm[q * LANES : (q + 1) * LANES, pl.ds(start, LANES)] = jnp.where(
                column - start == lane_perm, 1.0, 0.0
            ).astype(BF16)
            return carry

        lax.fori_loop(0, perm.shape[1] // LANES, build, 0)
    snaps[...] = jnp.zeros_like(snaps)

    first = add_shared(first, 0)
    axis_row = jnp.bitwise_and(row16, 3) < 3
    source = jnp.where(axis_row, first, 0.0)
    total = jnp.concatenate(
        [jnp.broadcast_to(first[4 * b + 3 : 4 * b + 4, :], (4, LANES)) for b in range(blocks)],
        axis=0,
    )
    half_inverse = jnp.where(axis_row, time_step / total, 0.0)

    low = [jnp.bitwise_and(conn_ref[8 * i : 8 * i + 8, :], LANES - 1) for i in range(3)]
    high = [jnp.right_shift(conn_ref[8 * i : 8 * i + 8, :], 7) for i in range(3)]

    def gradient(u):
        sides = []
        for c in range(3):
            rows = []
            for i in range(3):
                acc = None
                for b in range(blocks):
                    r = 4 * b + c
                    val = pick_lanes(jnp.broadcast_to(u[r : r + 1, :], (8, LANES)), low[i])
                    acc = val if b == 0 else jnp.where(high[i] == b, val, acc)
                rows.append(acc)
            rows.append(jnp.zeros((8, LANES), F32))
            hi, lo = split(jnp.concatenate(rows, axis=0))
            sides.append(jnp.concatenate([hi, lo, hi], axis=0))
        along = jnp.dot(
            w1[...], jnp.concatenate(sides, axis=1), preferred_element_type=F32
        )
        tensor = []
        for c in range(3):
            ref_dir = [
                along[r * points : (r + 1) * points, c * LANES : (c + 1) * LANES]
                for r in range(3)
            ]
            tensor.append(
                [
                    ref_dir[0] * jac_ref[e : e + 1, :]
                    + ref_dir[1] * jac_ref[3 + e : 4 + e, :]
                    + ref_dir[2] * jac_ref[6 + e : 7 + e, :]
                    for e in range(3)
                ]
            )
        return tensor

    def internal_force(t):
        lam = lame_ref[0:1, :]
        mu = lame_ref[1:2, :]
        pressure = lam * (t[0][0] + t[1][1] + t[2][2])
        stress = [[None] * 3 for _ in range(3)]
        for c in range(3):
            for e in range(c, 3):
                s = mu * (t[c][e] + t[e][c])
                if c == e:
                    s = s + pressure
                stress[c][e] = s
                stress[e][c] = s
        weight = pw_ref[...]
        highs = []
        lows = []
        for c in range(3):
            for r in range(3):
                m = stress[c][0] * jac_ref[3 * r : 3 * r + 1, :]
                m = m + stress[c][1] * jac_ref[3 * r + 1 : 3 * r + 2, :]
                m = m + stress[c][2] * jac_ref[3 * r + 2 : 3 * r + 3, :]
                hi, lo = split(m * weight)
                highs.append(hi)
                lows.append(lo)
        side = jnp.concatenate(highs + lows + highs, axis=0)
        values = jnp.dot(w2[...], side, preferred_element_type=F32)
        return scatter(lambda n: values[8 * n : 8 * n + 8, :])

    def record(t, slot_index):
        comps = [
            t[0][0],
            t[1][1],
            t[2][2],
            0.5 * (t[1][2] + t[2][1]),
            0.5 * (t[0][2] + t[2][0]),
            0.5 * (t[0][1] + t[1][0]),
        ]
        for c, value in enumerate(comps):
            start = pl.multiple_of(slot_index * (8 * points) + c * points, points)
            snaps[pl.ds(start, points), :] = value

    velocity = wav_ref[0] * source * half_inverse
    displace = time_step * velocity

    def advance(t, state):
        displace, velocity = state
        slot = lax.rem(t, 2)
        tensor = gradient(displace)
        force = wav_ref[t] * source
        inner = internal_force(tensor)
        send_shared(inner, slot)
        record(tensor, t - 1)
        inner = add_shared(inner, slot)
        velocity = velocity + half_inverse * (force - inner)
        displace = displace + time_step * velocity
        return displace, velocity

    displace, velocity = lax.fori_loop(1, steps, advance, (displace, velocity))
    record(gradient(displace), steps - 1)

    rows_all = steps * 8
    for q in range(points):
        lhs[:, q * LANES : (q + 1) * LANES] = snaps[
            pl.ds(q, rows_all, stride=points), :
        ].astype(BF16)

    def order_for(w):
        start = pl.multiple_of(w * block, block)
        res = jnp.dot(lhs[...], perm[:, pl.ds(start, block)], preferred_element_type=F32)
        return res.reshape(steps, 8, block)[:, 0:6, :].astype(BF16)

    def mine(i):
        return pl.ds(pl.multiple_of(i * block, block), block)

    sends = []
    for i in range(1, writers):
        w = lax.rem(d + i, writers)
        ordered[i] = order_for(w)
        copy = pltpu.make_async_remote_copy(
            src_ref=ordered.at[i],
            dst_ref=out_ref.at[:, :, mine(d)],
            send_sem=out_send_sem.at[i],
            recv_sem=out_recv_sem.at[i],
            device_id=(g, w),
            device_id_type=MESH,
        )
        copy.start()
        sends.append(copy)
    out_ref[:, :, mine(d)] = order_for(d)
    for i in range(1, writers):
        origin = lax.rem(d - i + writers, writers)
        pltpu.make_async_remote_copy(
            src_ref=ordered.at[i],
            dst_ref=out_ref.at[:, :, mine(origin)],
            send_sem=out_send_sem.at[i],
            recv_sem=out_recv_sem.at[i],
            device_id=(g, origin),
            device_id_type=MESH,
        ).wait_recv()
    for copy in sends:
        copy.wait_send()


def solution(mesh):
    groups, writers = mesh.shape["grp"], mesh.shape["dom"]

    def shards(
        connect,
        interface_nodes,
        neighbours,
        point_rank,
        shape_grad,
        inverse_jacobian,
        lame_moduli,
        point_weights,
        mass_elem,
        source_pattern,
        wavelet,
    ):
        nodes_el, elements = connect.shape
        points = point_weights.shape[0]
        point_count = point_rank.shape[1]
        steps = wavelet.shape[0]
        faces = interface_nodes[0]
        facet = faces.reshape(-1, 1)
        facesw = faces[jnp.array([1, 0, 3, 2])].reshape(1, -1)
        conn = jnp.pad(connect, ((0, 24 - nodes_el), (0, 0)))
        rankt = point_rank.reshape(points, elements).T
        w1f = jnp.tile(jnp.pad(shape_grad, ((0, 0), (0, 32 - nodes_el))), (1, 3))
        chan = jnp.arange(8)[:, None] % 4 == jnp.arange(3)[None, :]
        w2f = jnp.where(
            chan[None, :, None, :, None], shape_grad.T[:, None, None, None, :], 0.0
        )
        w2f = jnp.broadcast_to(w2f, (nodes_el, 8, 3, 3, 3 * points))
        w2f = w2f.reshape(nodes_el * 8, 27 * points)
        vmem = pl.BlockSpec(memory_space=pltpu.VMEM)
        smem = pl.BlockSpec(memory_space=pltpu.SMEM)
        return pl.pallas_call(
            functools.partial(kernel, groups, writers, steps, nodes_el),
            out_shape=jax.ShapeDtypeStruct((steps, 6, point_count), BF16),
            in_specs=[vmem] * 13 + [smem],
            out_specs=vmem,
            scratch_shapes=[
                pltpu.VMEM((nodes_el * LANES, LANES), BF16),
                pltpu.VMEM((nodes_el * 16, LANES), BF16),
                pltpu.VMEM((point_count, point_count), BF16),
                pltpu.VMEM(w1f.shape, BF16),
                pltpu.VMEM(w2f.shape, BF16),
                pltpu.VMEM((steps * 8 * points, LANES), F32),
                pltpu.VMEM((steps * 8, point_count), BF16),
                pltpu.VMEM((writers, steps, 6, point_count // writers), BF16),
                pltpu.VMEM((2, 8, LANES), F32),
                pltpu.VMEM((2, 4, 8, LANES), F32),
                pltpu.SemaphoreType.DMA((2, 4)),
                pltpu.SemaphoreType.DMA((2, 4)),
                pltpu.SemaphoreType.DMA((writers,)),
                pltpu.SemaphoreType.DMA((writers,)),
            ],
            compiler_params=pltpu.CompilerParams(
                collective_id=0, has_side_effects=True, vmem_limit_bytes=56 * 1024 * 1024
            ),
            name="window",
        )(
            conn,
            connect.T,
            facet,
            facesw,
            neighbours,
            rankt,
            w1f,
            w2f,
            inverse_jacobian,
            lame_moduli,
            point_weights,
            mass_elem,
            source_pattern,
            wavelet,
        )

    placed = (
        P(None, ("grp", "dom")),
        P(("grp", "dom"), None, None),
        P(("grp", "dom"), None),
        P(("grp", "dom"), None),
        P(),
        P(None, ("grp", "dom")),
        P(None, ("grp", "dom")),
        P(None, ("grp", "dom")),
        P(None, ("grp", "dom")),
        P(None, ("grp", "dom")),
        P(),
    )
    return jax.shard_map(
        shards, mesh=mesh, in_specs=placed, out_specs=P(None, None, ("grp", "dom")), check_vma=False
    )
```

time: 459 us -> 104 us (0.23); the launches traced: 453 us -> 104 us
  starting transfers between devices: 213 us -> 0 us
  Pallas kernels: 0 us -> 94.6 us
  matrix products: 90.2 us -> 0 us
  local copies, waits for them, and re-layouts: 77.7 us -> 8.04 us
  other arithmetic: 44.4 us -> 0.92 us
  waiting for transfers between devices: 12.1 us -> 0 us
  blocking collectives: 10.4 us -> 0 us
  loops' own time: 4.88 us -> 0 us
    ppermute x68 -> x0, starting transfers between devices: 213 us -> none  [the longest x34 169 us: extended(): lax.ppermute(tail, axis, [(i, (i + 1) % count) for i in range(ends)])]
    pallas_call x0 -> x1, Pallas kernels: none -> 94.6 us  [shards(): pl.pallas_call(functools.partial(kernel, groups, writers, steps, nodes_el...]
    dot_general x65 -> x0, matrix products: 90.2 us -> none  [the longest x16 48.8 us: gather_nodes(): lax.dot_general(displace, incidence.astype(jnp.float32), (((1,), (1,)), (...]
    gather x35 -> x1, local copies, waits for them, and re-layouts: 30.2 us -> 0.56 us  [shards(): facesw = faces[jnp.array([1, 0, 3, 2])].reshape(1, -1)]
    scatter-add x17 -> x0, other arithmetic: 23.2 us -> none  [assemble(): node_field.at[:, shared_nodes].add(received * neighbour_mask[None, :, None])]
    ppermute x68 -> x0, waiting for transfers between devices: 12.1 us -> none  [the longest x34 12 us: extended(): lax.ppermute(tail, axis, [(i, (i + 1) % count) for i in range(ends)])]
    unnamed x4 -> x0, other arithmetic: 10.9 us -> none
    all_to_all x1 -> x0, blocking collectives: 10.4 us -> none  [shards(): lax.all_to_all(ordered, 'dom', split_axis=2, concat_axis=2, tiled=True)]
  transfers between devices with their start and end apart: 68 -> 0, of which waited for: 16 -> 0; matrix products, arithmetic and copies ran while one was open for 2% -> 0% of each run, Pallas kernels for 0% -> 0%
where the time goes in v1:
time: 104 us
  Pallas kernels  94.6 us (91%)
  local copies, waits for them, and re-layouts  8.04 us (8%)
    pallas_call x1, Pallas kernels, shards(): pl.pallas_call(functools.partial(kernel, groups, writers, steps, nodes_el...  94.6 us

profile of v1, /device:TPU:0, one launch (start us, length us, event | category | flops | bytes accessed | tf_op | source)
XLA Modules:
  0.0 103.6 jit_solution(10499922113784807430)
XLA Ops:
  0.0 0.1 iota_compare_fusion
  0.1 0.8 broadcast_select_fusion
  0.9 0.1 broadcast_in_dim.36
  1.1 0.0 copy-start.2
  1.1 1.2 %reshape.59.w2f_ref = f32[160,432]{1,0:T(8,128)} reshape(f32[20,8,3,3,48]{4,3,2,1,0:T(4,128)S(1)} %broadcast_in_dim.36) | data formatting | bytes 552960 | tf_op jit(solution)/shard_map/reshape | solution.py:389
  2.2 0.0 copy-done.2
  2.3 0.0 copy-start.1
  2.3 0.7 copy.20.w1f_ref
  3.0 0.0 copy-done.1
  3.0 0.0 copy-start.3
  3.0 0.7 copy.17
  3.7 0.0 copy-done.3
  3.7 0.0 copy-start
  3.7 0.7 copy.18
  4.4 0.0 copy-done
  4.4 0.7 reshape_squeeze.4.facet_ref
  5.2 0.0 copy-start.4
  5.2 0.6 pad.8.conn_ref
  5.8 0.1 copy-done.4
  5.8 0.6 gather_fusion
  6.4 0.6 reshape.57.facesw_ref
  7.0 94.6 %window.1 = bf16[16,6,2048]{2,1,0:T(8,128)(2,1)} custom-call(s32[24,128]{1,0:T(8,128)} %pad.8.conn_ref, s32[128,20]{1,0:T(8,128)} %bitcast.6, s32[128,1]{1,0:T(8,128)} %reshape_squeeze.4.facet_ref, s32[1,128]{1,0:T(1,128)} %reshape.57.facesw_ref, s32[1,4]{1,0:T(1,128)} %nb_ref.1, s32[128,16]{1,0:T(8,128)} %bitcast.7, f32[48,96]{1,0:T(8,128)} %copy.20.w1f_ref, ...), custom_call_target="tpu_custom_call" | custom-call | tf_op jit(solution)/shard_map/window/pallas_call | solution.py:392
  101.6 2.0 %copy.21 = bf16[16,6,2048]{2,0,1:T(8,128)(2,1)} copy(bf16[16,6,2048]{2,1,0:T(8,128)(2,1)} %window.1) | data formatting | bytes 786432 | tf_op jit(solution)/shard_map/window/pallas_call | solution.py:392
  (4 shorter events, 0.0 us)
Async XLA Ops:
  1.1 1.2 %copy-start.2 = (f32[48,20]{0,1:T(8,128)S(1)}, f32[48,20]{0,1:T(8,128)}, u32[]{:S(2)}) copy-start(f32[48,20]{0,1:T(8,128)} %param.16) | copy-start | bytes 11524
  2.3 0.7 copy-start.1
  3.0 0.7 copy-start.3
  3.7 0.7 copy-start
  5.2 0.7 copy-start.4

commit v2 on v1

--- a/solution.py
+++ b/solution.py
@@ -29,13 +29,10 @@
     steps,
     nodes_el,
     conn_ref,
-    connt_ref,
-    facet_ref,
-    facesw_ref,
+    faces_ref,
     nb_ref,
-    rankt_ref,
-    w1f_ref,
-    w2f_ref,
+    rank_ref,
+    gradt_ref,
     jac_ref,
     lame_ref,
     pw_ref,
@@ -80,32 +77,52 @@
             barrier, inc=1, device_id=(g, lax.rem(d + i, writers)), device_id_type=MESH
         )
 
-    lane128 = lax.broadcasted_iota(jnp.int32, (LANES, LANES), 1)
+    lane = lax.broadcasted_iota(jnp.int32, (LANES, LANES), 1)
     row16 = lax.broadcasted_iota(jnp.int32, (16, LANES), 0)
+    conn_low = jnp.bitwise_and(conn_ref[...], LANES - 1)
+    conn_high = jnp.right_shift(conn_ref[...], 7)
+    columns = jnp.concatenate(
+        [conn_low.astype(F32), jnp.zeros((LANES - nodes_el, LANES), F32)], axis=0
+    ).T
     for n in range(nodes_el):
-        low = jnp.bitwise_and(connt_ref[:, n : n + 1], LANES - 1)
-        onehot[n * LANES : (n + 1) * LANES, :] = jnp.where(low == lane128, 1.0, 0.0).astype(BF16)
-        high = jnp.right_shift(conn_ref[n : n + 1, :], 7)
+        hit = jnp.where(columns[:, n : n + 1] == lane.astype(F32), 1.0, 0.0)
+        onehot[n * LANES : (n + 1) * LANES, :] = hit.astype(BF16)
         hmask[n * 16 : (n + 1) * 16, :] = jnp.where(
-            high == jnp.right_shift(row16, 2), 1.0, 0.0
+            conn_high[n : n + 1, :] == jnp.right_shift(row16, 2), 1.0, 0.0
         ).astype(BF16)
-    for ref, full in ((w1, w1f_ref), (w2, w2f_ref)):
-        hi, lo = split(full[...])
-        col = lax.broadcasted_iota(jnp.int32, full.shape, 1)
-        ref[...] = jnp.where(
-            col < (full.shape[1] // 3) * 2, hi.astype(F32), lo.astype(F32)
-        ).astype(BF16)
-
-    facesw = facesw_ref[...]
-    face_low = jnp.broadcast_to(jnp.bitwise_and(facesw, LANES - 1), (8, LANES))
+    gradt = gradt_ref[...]
+    depth = 3 * points
+    hi = gradt.astype(BF16).astype(F32)
+    lo = gradt - hi
+    gap = jnp.zeros((32 - nodes_el, depth), F32)
+    tall = jnp.concatenate([hi, gap, hi, gap, lo, gap, jnp.zeros((32, depth), F32)], axis=0)
+    tall = jnp.concatenate([tall, jnp.zeros((LANES, LANES - depth), F32)], axis=1)
+    w1[...] = tall.T[0:depth, 0:96].astype(BF16)
+    wide = jnp.concatenate([hi] * 6 + [lo] * 3, axis=1)
+    col = lax.broadcasted_iota(jnp.int32, (8, 9 * depth), 1)
+    rows = jnp.bitwise_and(lax.broadcasted_iota(jnp.int32, (8, 9 * depth), 0), 3)
+    own = (col >= rows * depth) & (col < (rows + 1) * depth)
+    for piece in (3, 6):
+        own = own | ((col >= (rows + piece) * depth) & (col < (rows + piece + 1) * depth))
+    own = own & (rows < 3)
+    for n in range(0, nodes_el, 2):
+        two = [jnp.where(own, wide[m : m + 1, :], 0.0) for m in (n, n + 1)]
+        w2[n * 8 : n * 8 + 16, :] = jnp.concatenate(two, axis=0).astype(BF16)
+
+    faces = faces_ref[0].astype(F32)
+    face_row = jnp.concatenate([faces[k : k + 1, :] for k in range(4)], axis=1)
+    face_swap = jnp.concatenate([faces[k ^ 1 : (k ^ 1) + 1, :] for k in range(4)], axis=1)
+    face_swap = face_swap.astype(jnp.int32)
+    face_low = jnp.broadcast_to(jnp.bitwise_and(face_swap, LANES - 1), (8, LANES))
     face_mask = jnp.where(
-        jnp.right_shift(facesw, 7) == jnp.right_shift(row16, 2), 1.0, 0.0
+        jnp.right_shift(face_swap, 7) == jnp.right_shift(row16, 2), 1.0, 0.0
     )
+    face_col = jnp.broadcast_to(face_row, (LANES, LANES)).T
     position = lax.broadcasted_iota(jnp.int32, (LANES, LANES), 0).astype(F32)
     inv_rows = []
     has_rows = []
     for b in range(blocks):
-        hit = jnp.where(facet_ref[...] == lane128 + b * LANES, 1.0, 0.0)
+        hit = jnp.where(face_col == (lane + b * LANES).astype(F32), 1.0, 0.0)
         inv_rows.append(
             jnp.broadcast_to(jnp.sum(hit * position, axis=0, keepdims=True), (4, LANES))
         )
@@ -194,19 +211,16 @@
     )
     send_shared(first, 0)
 
-    lane_perm = lax.broadcasted_iota(jnp.int32, (LANES, LANES), 1)
-    for q in range(points):
-        column = rankt_ref[:, q : q + 1]
-
-        def build(j, carry):
-            start = pl.multiple_of(j * LANES, LANES)
-            perm[q * LANES : (q + 1) * LANES, pl.ds(start, LANES)] = jnp.where(
-                column - start == lane_perm, 1.0, 0.0
-            ).astype(BF16)
-            return carry
-
-        lax.fori_loop(0, perm.shape[1] // LANES, build, 0)
-    snaps[...] = jnp.zeros_like(snaps)
+    rank_row = lax.broadcasted_iota(jnp.int32, (perm.shape[0], LANES), 0)
+
+    def build_order(q):
+        start = pl.multiple_of(q * LANES, LANES)
+        perm[:, pl.ds(start, LANES)] = jnp.where(
+            rank_ref[:, pl.ds(start, LANES)] == rank_row, 1.0, 0.0
+        ).astype(BF16)
+
+    for q in range(max(points - steps + 1, 0)):
+        build_order(q)
 
     first = add_shared(first, 0)
     axis_row = jnp.bitwise_and(row16, 3) < 3
@@ -217,8 +231,11 @@
     )
     half_inverse = jnp.where(axis_row, time_step / total, 0.0)
 
-    low = [jnp.bitwise_and(conn_ref[8 * i : 8 * i + 8, :], LANES - 1) for i in range(3)]
-    high = [jnp.right_shift(conn_ref[8 * i : 8 * i + 8, :], 7) for i in range(3)]
+    spare = jnp.zeros((24 - nodes_el, LANES), jnp.int32)
+    conn_low = jnp.concatenate([conn_low, spare], axis=0)
+    conn_high = jnp.concatenate([conn_high, spare], axis=0)
+    low = [conn_low[8 * i : 8 * i + 8, :] for i in range(3)]
+    high = [conn_high[8 * i : 8 * i + 8, :] for i in range(3)]
 
     def gradient(u):
         sides = []
@@ -290,7 +307,7 @@
             0.5 * (t[0][1] + t[1][0]),
         ]
         for c, value in enumerate(comps):
-            start = pl.multiple_of(slot_index * (8 * points) + c * points, points)
+            start = pl.multiple_of((c * steps + slot_index) * points, points)
             snaps[pl.ds(start, points), :] = value
 
     velocity = wav_ref[0] * source * half_inverse
@@ -304,6 +321,7 @@
         inner = internal_force(tensor)
         send_shared(inner, slot)
         record(tensor, t - 1)
+        build_order(t + (points - steps))
         inner = add_shared(inner, slot)
         velocity = velocity + half_inverse * (force - inner)
         displace = displace + time_step * velocity
@@ -312,7 +330,7 @@
     displace, velocity = lax.fori_loop(1, steps, advance, (displace, velocity))
     record(gradient(displace), steps - 1)
 
-    rows_all = steps * 8
+    rows_all = steps * 6
     for q in range(points):
         lhs[:, q * LANES : (q + 1) * LANES] = snaps[
             pl.ds(q, rows_all, stride=points), :
@@ -320,8 +338,13 @@
 
     def order_for(w):
         start = pl.multiple_of(w * block, block)
-        res = jnp.dot(lhs[...], perm[:, pl.ds(start, block)], preferred_element_type=F32)
-        return res.reshape(steps, 8, block)[:, 0:6, :].astype(BF16)
+        res = lax.dot_general(
+            lhs[...],
+            perm[pl.ds(start, block), :],
+            (((1,), (1,)), ((), ())),
+            preferred_element_type=F32,
+        )
+        return res.astype(BF16).reshape(6, steps, block)
 
     def mine(i):
         return pl.ds(pl.multiple_of(i * block, block), block)
@@ -375,34 +398,22 @@
         points = point_weights.shape[0]
         point_count = point_rank.shape[1]
         steps = wavelet.shape[0]
-        faces = interface_nodes[0]
-        facet = faces.reshape(-1, 1)
-        facesw = faces[jnp.array([1, 0, 3, 2])].reshape(1, -1)
-        conn = jnp.pad(connect, ((0, 24 - nodes_el), (0, 0)))
-        rankt = point_rank.reshape(points, elements).T
-        w1f = jnp.tile(jnp.pad(shape_grad, ((0, 0), (0, 32 - nodes_el))), (1, 3))
-        chan = jnp.arange(8)[:, None] % 4 == jnp.arange(3)[None, :]
-        w2f = jnp.where(
-            chan[None, :, None, :, None], shape_grad.T[:, None, None, None, :], 0.0
-        )
-        w2f = jnp.broadcast_to(w2f, (nodes_el, 8, 3, 3, 3 * points))
-        w2f = w2f.reshape(nodes_el * 8, 27 * points)
         vmem = pl.BlockSpec(memory_space=pltpu.VMEM)
         smem = pl.BlockSpec(memory_space=pltpu.SMEM)
-        return pl.pallas_call(
+        ordered = pl.pallas_call(
             functools.partial(kernel, groups, writers, steps, nodes_el),
-            out_shape=jax.ShapeDtypeStruct((steps, 6, point_count), BF16),
-            in_specs=[vmem] * 13 + [smem],
+            out_shape=jax.ShapeDtypeStruct((6, steps, point_count), BF16),
+            in_specs=[vmem] * 10 + [smem],
             out_specs=vmem,
             scratch_shapes=[
                 pltpu.VMEM((nodes_el * LANES, LANES), BF16),
                 pltpu.VMEM((nodes_el * 16, LANES), BF16),
                 pltpu.VMEM((point_count, point_count), BF16),
-                pltpu.VMEM(w1f.shape, BF16),
-                pltpu.VMEM(w2f.shape, BF16),
-                pltpu.VMEM((steps * 8 * points, LANES), F32),
-                pltpu.VMEM((steps * 8, point_count), BF16),
-                pltpu.VMEM((writers, steps, 6, point_count // writers), BF16),
+                pltpu.VMEM((3 * points, 96), BF16),
+                pltpu.VMEM((nodes_el * 8, 27 * points), BF16),
+                pltpu.VMEM((steps * 6 * points, LANES), F32),
+                pltpu.VMEM((steps * 6, point_count), BF16),
+                pltpu.VMEM((writers, 6, steps, point_count // writers), BF16),
                 pltpu.VMEM((2, 8, LANES), F32),
                 pltpu.VMEM((2, 4, 8, LANES), F32),
                 pltpu.SemaphoreType.DMA((2, 4)),
@@ -415,14 +426,11 @@
             ),
             name="window",
         )(
-            conn,
-            connect.T,
-            facet,
-            facesw,
+            connect,
+            interface_nodes,
             neighbours,
-            rankt,
-            w1f,
-            w2f,
+            point_rank,
+            shape_grad.T,
             inverse_jacobian,
             lame_moduli,
             point_weights,
@@ -430,6 +438,7 @@
             source_pattern,
             wavelet,
         )
+        return ordered.transpose(1, 0, 2)
 
     placed = (
         P(None, ("grp", "dom")),

time: 104 us -> 75.8 us (0.73)
  Pallas kernels: 94.6 us -> 73.9 us
  local copies, waits for them, and re-layouts: 8.04 us -> 1.77 us
    pallas_call x1, Pallas kernels: 94.6 us -> 73.9 us  [shards(): pl.pallas_call(functools.partial(kernel, groups, writers, steps, nodes_el...]
    reshape x3 -> x0, local copies, waits for them, and re-layouts: 2.5 us -> none  [the longest x1 1.16 us: shards(): w2f = w2f.reshape(nodes_el * 8, 27 * points)]
    pallas_call x1 -> x0, local copies, waits for them, and re-layouts: 2.01 us -> none  [shards(): pl.pallas_call(functools.partial(kernel, groups, writers, steps, nodes_el...]
    another operation x3 -> x0, local copies, waits for them, and re-layouts: 1.41 us -> none  [the longest x1 0.72 us: shards(): facet = faces.reshape(-1, 1)]
where the time goes in v2:
time: 75.8 us; the launch traced here: 75.6 us
  Pallas kernels  73.9 us (97%)
  local copies, waits for them, and re-layouts  1.77 us (2%)
    pallas_call x1, Pallas kernels, shards(): pl.pallas_call(functools.partial(kernel, groups, writers, steps, nodes_el...  73.9 us
    unnamed x1, local copies, waits for them, and re-layouts  1.77 us

profile of v2, /device:TPU:0, one launch (start us, length us, event | category | flops | bytes accessed | tf_op | source)
XLA Modules:
  0.0 75.6 jit_solution(7346014382966666239)
XLA Ops:
  0.0 73.9 %window.1 = bf16[6,16,2048]{2,1,0:T(8,128)(2,1)} custom-call(s32[20,128]{1,0:T(8,128)} %conn_ref.1, s32[1,4,32]{2,1,0:T(4,128)} %faces_ref.1, s32[1,4]{1,0:T(1,128)} %nb_ref.1, s32[1,2048]{1,0:T(1,128)} %rank_ref.1, f32[20,48]{1,0:T(8,128)} %bitcast.3, f32[9,128]{1,0:T(8,128)} %jac_ref.1, f32[2,128]{1,0:T(2,128)} %lame_ref.1, f32[16,128]{1,0:T(8,128)} %pw_ref.1, ...), custom_call_target="tpu_custom_call" | custom-call | tf_op jit(solution)/shard_map/window/pallas_call | solution.py:403
  73.9 1.8 %copy.13 = bf16[16,6,2048]{2,0,1:T(8,128)(2,1)} copy(bf16[16,6,2048]{2,0,1:T(8,128)(2,1)} %bitcast.2) | data formatting | bytes 786432

commit v3 on v2

--- a/solution.py
+++ b/solution.py
@@ -79,14 +79,38 @@
 
     lane = lax.broadcasted_iota(jnp.int32, (LANES, LANES), 1)
     row16 = lax.broadcasted_iota(jnp.int32, (16, LANES), 0)
+    faces = faces_ref[0].astype(F32)
+    face_row = jnp.concatenate([faces[k : k + 1, :] for k in range(4)], axis=1)
+    face_swap = jnp.concatenate([faces[k ^ 1 : (k ^ 1) + 1, :] for k in range(4)], axis=1)
+    face_swap = face_swap.astype(jnp.int32)
+    face_low = jnp.broadcast_to(jnp.bitwise_and(face_swap, LANES - 1), (8, LANES))
+    face_mask = jnp.where(
+        jnp.right_shift(face_swap, 7) == jnp.right_shift(row16, 2), 1.0, 0.0
+    )
+    face_col = jnp.broadcast_to(face_row, (LANES, LANES)).T
+    position = lax.broadcasted_iota(jnp.int32, (LANES, LANES), 0).astype(F32)
+    inv_rows = []
+    has_rows = []
+    for b in range(blocks):
+        hit = jnp.where(face_col == (lane + b * LANES).astype(F32), 1.0, 0.0)
+        inv_rows.append(
+            jnp.broadcast_to(jnp.sum(hit * position, axis=0, keepdims=True), (4, LANES))
+        )
+        has_rows.append(jnp.broadcast_to(jnp.sum(hit, axis=0, keepdims=True), (4, LANES)))
+    inv_idx = jnp.concatenate(inv_rows, axis=0).astype(jnp.int32)
+    inv_has = jnp.concatenate(has_rows, axis=0)
+
     conn_low = jnp.bitwise_and(conn_ref[...], LANES - 1)
     conn_high = jnp.right_shift(conn_ref[...], 7)
     columns = jnp.concatenate(
         [conn_low.astype(F32), jnp.zeros((LANES - nodes_el, LANES), F32)], axis=0
     ).T
     for n in range(nodes_el):
-        hit = jnp.where(columns[:, n : n + 1] == lane.astype(F32), 1.0, 0.0)
-        onehot[n * LANES : (n + 1) * LANES, :] = hit.astype(BF16)
+        here = jnp.broadcast_to(columns[:, n : n + 1], (LANES, LANES))
+        hit = jnp.where(here == lane.astype(F32), 1.0, 0.0)
+        onehot[n * LANES : (n + 1) * LANES, 0:LANES] = hit.astype(BF16)
+        hit = jnp.where(here == face_low[0:1, :].astype(F32), 1.0, 0.0)
+        onehot[n * LANES : (n + 1) * LANES, LANES:] = hit.astype(BF16)
         hmask[n * 16 : (n + 1) * 16, :] = jnp.where(
             conn_high[n : n + 1, :] == jnp.right_shift(row16, 2), 1.0, 0.0
         ).astype(BF16)
@@ -109,26 +133,6 @@
         two = [jnp.where(own, wide[m : m + 1, :], 0.0) for m in (n, n + 1)]
         w2[n * 8 : n * 8 + 16, :] = jnp.concatenate(two, axis=0).astype(BF16)
 
-    faces = faces_ref[0].astype(F32)
-    face_row = jnp.concatenate([faces[k : k + 1, :] for k in range(4)], axis=1)
-    face_swap = jnp.concatenate([faces[k ^ 1 : (k ^ 1) + 1, :] for k in range(4)], axis=1)
-    face_swap = face_swap.astype(jnp.int32)
-    face_low = jnp.broadcast_to(jnp.bitwise_and(face_swap, LANES - 1), (8, LANES))
-    face_mask = jnp.where(
-        jnp.right_shift(face_swap, 7) == jnp.right_shift(row16, 2), 1.0, 0.0
-    )
-    face_col = jnp.broadcast_to(face_row, (LANES, LANES)).T
-    position = lax.broadcasted_iota(jnp.int32, (LANES, LANES), 0).astype(F32)
-    inv_rows = []
-    has_rows = []
-    for b in range(blocks):
-        hit = jnp.where(face_col == (lane + b * LANES).astype(F32), 1.0, 0.0)
-        inv_rows.append(
-            jnp.broadcast_to(jnp.sum(hit * position, axis=0, keepdims=True), (4, LANES))
-        )
-        has_rows.append(jnp.broadcast_to(jnp.sum(hit, axis=0, keepdims=True), (4, LANES)))
-    inv_idx = jnp.concatenate(inv_rows, axis=0).astype(jnp.int32)
-    inv_has = jnp.concatenate(has_rows, axis=0)
     quarter = jnp.right_shift(lax.broadcasted_iota(jnp.int32, (8, LANES), 1), 5)
     nb = nb_ref[...].astype(F32)
     recv_mask = [jnp.where(quarter == k, nb[:, k : k + 1], 0.0) for k in range(4)]
@@ -160,8 +164,8 @@
         ]
 
     def send_shared(field, slot):
-        part = pick_lanes(field[0:8], face_low) * face_mask[0:8]
-        part = part + pick_lanes(field[8:16], face_low) * face_mask[8:16]
+        part = field[:, LANES:] * face_mask
+        part = part[0:8] + part[8:16]
         send[slot] = part + pltpu.roll(part, 4, 0)
         for k, copy in enumerate(copies(slot)):
 
@@ -169,7 +173,7 @@
             def _():
                 copy.start()
 
-    def add_shared(field, slot):
+    def shared_sum(slot):
         for k, copy in enumerate(arrivals(slot)):
 
             @pl.when(has[k])
@@ -180,10 +184,13 @@
         got = recv[slot, 0] * recv_mask[0]
         for k in range(1, 4):
             got = got + recv[slot, k] * recv_mask[k]
+        return got
+
+    def at_nodes(got):
         added = jnp.concatenate(
             [pick_lanes(got, inv_idx[0:8]), pick_lanes(got, inv_idx[8:16])], axis=0
         )
-        return field + added * inv_has
+        return added * inv_has
 
     def scatter(rows):
         pieces = []
@@ -204,7 +211,11 @@
     for b in range(blocks):
         src_rows.append(src_ref[:, b * LANES : (b + 1) * LANES])
         src_rows.append(jnp.zeros((1, LANES), F32))
-    first = mass + jnp.concatenate(src_rows, axis=0)
+    source_rows = jnp.concatenate(src_rows, axis=0)
+    source_low = jnp.concatenate(
+        [pick_lanes(source_rows[i : i + 8], face_low) for i in (0, 8)], axis=0
+    )
+    first = mass + jnp.concatenate([source_rows, source_low], axis=1)
 
     pl.semaphore_wait(
         barrier, has[0].astype(jnp.int32) + has[1].astype(jnp.int32) + writers - 1
@@ -219,10 +230,12 @@
             rank_ref[:, pl.ds(start, LANES)] == rank_row, 1.0, 0.0
         ).astype(BF16)
 
-    for q in range(max(points - steps + 1, 0)):
+    half = steps // 2
+    tables = -(-points // half)
+    for q in range(min(tables, points)):
         build_order(q)
 
-    first = add_shared(first, 0)
+    first = first[:, 0:LANES] + at_nodes(shared_sum(0))
     axis_row = jnp.bitwise_and(row16, 3) < 3
     source = jnp.where(axis_row, first, 0.0)
     total = jnp.concatenate(
@@ -237,18 +250,39 @@
     low = [conn_low[8 * i : 8 * i + 8, :] for i in range(3)]
     high = [conn_high[8 * i : 8 * i + 8, :] for i in range(3)]
 
-    def gradient(u):
+    def at_elements(rows_of):
+        out = []
+        for i in range(3):
+            acc = None
+            for b in range(blocks):
+                val = pick_lanes(jnp.broadcast_to(rows_of(b), (8, LANES)), low[i])
+                acc = val if b == 0 else jnp.where(high[i] == b, val, acc)
+            out.append(acc)
+        return out
+
+    inv_f = inv_idx.astype(F32)
+    place = [x.astype(jnp.int32) for x in at_elements(lambda b: inv_f[4 * b : 4 * b + 1, :])]
+    coef = (-time_step) * half_inverse * inv_has
+    coef = at_elements(lambda b: coef[4 * b : 4 * b + 1, :])
+
+    def gather(u):
+        return tuple(
+            tuple(at_elements(lambda b: u[4 * b + c : 4 * b + c + 1, :])) for c in range(3)
+        )
+
+    def corrected(values, got):
+        out = []
+        for c in range(3):
+            row = jnp.broadcast_to(got[c : c + 1, :], (8, LANES))
+            out.append(
+                tuple(values[c][i] + pick_lanes(row, place[i]) * coef[i] for i in range(3))
+            )
+        return tuple(out)
+
+    def gradient(values):
         sides = []
         for c in range(3):
-            rows = []
-            for i in range(3):
-                acc = None
-                for b in range(blocks):
-                    r = 4 * b + c
-                    val = pick_lanes(jnp.broadcast_to(u[r : r + 1, :], (8, LANES)), low[i])
-                    acc = val if b == 0 else jnp.where(high[i] == b, val, acc)
-                rows.append(acc)
-            rows.append(jnp.zeros((8, LANES), F32))
+            rows = list(values[c]) + [jnp.zeros((8, LANES), F32)]
             hi, lo = split(jnp.concatenate(rows, axis=0))
             sides.append(jnp.concatenate([hi, lo, hi], axis=0))
         along = jnp.dot(
@@ -307,34 +341,12 @@
             0.5 * (t[0][1] + t[1][0]),
         ]
         for c, value in enumerate(comps):
-            start = pl.multiple_of((c * steps + slot_index) * points, points)
+            start = (slot_index // half) * 6 + c
+            start = pl.multiple_of((start * half + lax.rem(slot_index, half)) * points, points)
             snaps[pl.ds(start, points), :] = value
 
     velocity = wav_ref[0] * source * half_inverse
     displace = time_step * velocity
-
-    def advance(t, state):
-        displace, velocity = state
-        slot = lax.rem(t, 2)
-        tensor = gradient(displace)
-        force = wav_ref[t] * source
-        inner = internal_force(tensor)
-        send_shared(inner, slot)
-        record(tensor, t - 1)
-        build_order(t + (points - steps))
-        inner = add_shared(inner, slot)
-        velocity = velocity + half_inverse * (force - inner)
-        displace = displace + time_step * velocity
-        return displace, velocity
-
-    displace, velocity = lax.fori_loop(1, steps, advance, (displace, velocity))
-    record(gradient(displace), steps - 1)
-
-    rows_all = steps * 6
-    for q in range(points):
-        lhs[:, q * LANES : (q + 1) * LANES] = snaps[
-            pl.ds(q, rows_all, stride=points), :
-        ].astype(BF16)
 
     def order_for(w):
         start = pl.multiple_of(w * block, block)
@@ -344,38 +356,70 @@
             (((1,), (1,)), ((), ())),
             preferred_element_type=F32,
         )
-        return res.astype(BF16).reshape(6, steps, block)
+        return res.astype(BF16).reshape(6, half, block)
 
     def mine(i):
         return pl.ds(pl.multiple_of(i * block, block), block)
 
-    sends = []
-    for i in range(1, writers):
-        w = lax.rem(d + i, writers)
-        ordered[i] = order_for(w)
-        copy = pltpu.make_async_remote_copy(
-            src_ref=ordered.at[i],
-            dst_ref=out_ref.at[:, :, mine(d)],
-            send_sem=out_send_sem.at[i],
-            recv_sem=out_recv_sem.at[i],
-            device_id=(g, w),
+    def parcel(h, i, column, target):
+        return pltpu.make_async_remote_copy(
+            src_ref=ordered.at[h, i],
+            dst_ref=out_ref.at[:, h * half : (h + 1) * half, mine(column)],
+            send_sem=out_send_sem.at[h, i],
+            recv_sem=out_recv_sem.at[h, i],
+            device_id=(g, target),
             device_id_type=MESH,
         )
-        copy.start()
-        sends.append(copy)
-    out_ref[:, :, mine(d)] = order_for(d)
-    for i in range(1, writers):
-        origin = lax.rem(d - i + writers, writers)
-        pltpu.make_async_remote_copy(
-            src_ref=ordered.at[i],
-            dst_ref=out_ref.at[:, :, mine(origin)],
-            send_sem=out_send_sem.at[i],
-            recv_sem=out_recv_sem.at[i],
-            device_id=(g, origin),
-            device_id_type=MESH,
-        ).wait_recv()
-    for copy in sends:
-        copy.wait_send()
+
+    def ship(h):
+        count = 6 * half
+        for q in range(points):
+            lhs[:, q * LANES : (q + 1) * LANES] = snaps[
+                pl.ds(h * count * points + q, count, stride=points), :
+            ].astype(BF16)
+        for i in range(1, writers):
+            w = lax.rem(d + i, writers)
+            ordered[h, i] = order_for(w)
+            parcel(h, i, d, w).start()
+        out_ref[:, h * half : (h + 1) * half, mine(d)] = order_for(d)
+
+    def advance(t, state, extra):
+        values, displace, velocity = state
+        slot = lax.rem(t, 2)
+        tensor = gradient(values)
+        inner = internal_force(tensor)
+        send_shared(inner, slot)
+        velocity = velocity + half_inverse * (wav_ref[t] * source - inner[:, 0:LANES])
+        displace = displace + time_step * velocity
+        values = gather(displace)
+        record(tensor, t - 1)
+        extra(t)
+        got = shared_sum(slot)
+        values = corrected(values, got)
+        change = half_inverse * at_nodes(got)
+        return values, displace - time_step * change, velocity - change
+
+    def early(t, state):
+        def extra(t):
+            for i in range(tables):
+                build_order(jnp.minimum(t * tables + i, points - 1))
+
+        return advance(t, state, extra)
+
+    state = (gather(displace), displace, velocity)
+    state = lax.fori_loop(1, half, early, state)
+    state = advance(jnp.int32(half), state, lambda t: ship(0))
+    state = lax.fori_loop(
+        half + 1, steps, lambda t, held: advance(t, held, lambda t: None), state
+    )
+    record(gradient(state[0]), jnp.int32(steps - 1))
+    ship(1)
+    for h in range(2):
+        for i in range(1, writers):
+            origin = lax.rem(d - i + writers, writers)
+            parcel(h, i, origin, origin).wait_recv()
+            w = lax.rem(d + i, writers)
+            parcel(h, i, d, w).wait_send()
 
 
 def solution(mesh):
@@ -406,20 +450,20 @@
             in_specs=[vmem] * 10 + [smem],
             out_specs=vmem,
             scratch_shapes=[
-                pltpu.VMEM((nodes_el * LANES, LANES), BF16),
+                pltpu.VMEM((nodes_el * LANES, 2 * LANES), BF16),
                 pltpu.VMEM((nodes_el * 16, LANES), BF16),
                 pltpu.VMEM((point_count, point_count), BF16),
                 pltpu.VMEM((3 * points, 96), BF16),
                 pltpu.VMEM((nodes_el * 8, 27 * points), BF16),
                 pltpu.VMEM((steps * 6 * points, LANES), F32),
-                pltpu.VMEM((steps * 6, point_count), BF16),
-                pltpu.VMEM((writers, 6, steps, point_count // writers), BF16),
+                pltpu.VMEM((steps // 2 * 6, point_count), BF16),
+                pltpu.VMEM((2, writers, 6, steps // 2, point_count // writers), BF16),
                 pltpu.VMEM((2, 8, LANES), F32),
                 pltpu.VMEM((2, 4, 8, LANES), F32),
                 pltpu.SemaphoreType.DMA((2, 4)),
                 pltpu.SemaphoreType.DMA((2, 4)),
-                pltpu.SemaphoreType.DMA((writers,)),
-                pltpu.SemaphoreType.DMA((writers,)),
+                pltpu.SemaphoreType.DMA((2, writers)),
+                pltpu.SemaphoreType.DMA((2, writers)),
             ],
             compiler_params=pltpu.CompilerParams(
                 collective_id=0, has_side_effects=True, vmem_limit_bytes=56 * 1024 * 1024

time: 75.8 us -> 72.8 us (0.960)
  Pallas kernels: 73.9 us -> 70.8 us
    pallas_call x1, Pallas kernels: 73.9 us -> 70.8 us  [shards(): pl.pallas_call(functools.partial(kernel, groups, writers, steps, nodes_el...]
where the time goes in v3:
time: 72.8 us; the launch traced here: 72.6 us
  Pallas kernels  70.8 us (97%)
  local copies, waits for them, and re-layouts  1.77 us (2%)
    pallas_call x1, Pallas kernels, shards(): pl.pallas_call(functools.partial(kernel, groups, writers, steps, nodes_el...  70.8 us
    unnamed x1, local copies, waits for them, and re-layouts  1.77 us

profile of v3, /device:TPU:0, one launch (start us, length us, event | category | flops | bytes accessed | tf_op | source)
XLA Modules:
  0.0 72.6 jit_solution(11076968477568259354)
XLA Ops:
  0.0 70.8 %window.1 = bf16[6,16,2048]{2,1,0:T(8,128)(2,1)} custom-call(s32[20,128]{1,0:T(8,128)} %conn_ref.1, s32[1,4,32]{2,1,0:T(4,128)} %faces_ref.1, s32[1,4]{1,0:T(1,128)} %nb_ref.1, s32[1,2048]{1,0:T(1,128)} %rank_ref.1, f32[20,48]{1,0:T(8,128)} %bitcast.3, f32[9,128]{1,0:T(8,128)} %jac_ref.1, f32[2,128]{1,0:T(2,128)} %lame_ref.1, f32[16,128]{1,0:T(8,128)} %pw_ref.1, ...), custom_call_target="tpu_custom_call" | custom-call | tf_op jit(solution)/shard_map/window/pallas_call | solution.py:447
  70.8 1.8 %copy.13 = bf16[16,6,2048]{2,0,1:T(8,128)(2,1)} copy(bf16[16,6,2048]{2,0,1:T(8,128)(2,1)} %bitcast.2) | data formatting | bytes 786432
